TPU v7x, 128 devices: a 2x2x16 block of a 8x8x16 slice. The times are simulated.
128 devices in a mesh: mol: 4 (over y, x), pts: 32 (over z, core).
Axes of the slice: x: 2, y: 2, z: 16, core: 2. Of those that a mesh axis runs over, the one named last changes fastest.
The devices are a block of a 8x8x16 slice.
Arguments:
- points_map: bfloat16 [25600, 800], P(('mol', 'pts')), parts along dimension 0, may hold values from -0.21875 to 0.21875
- trial: bfloat16 [25600, 128], P('mol'), parts along dimension 0, may hold values from -6 to 6
- core: bfloat16 [25600, 6400], P(('mol', 'pts')), parts along dimension 0, may hold values from -2 to 4, as said below
- walkers: bfloat16 [3200, 12, 128], P('mol'), parts along dimension 0, may hold values from -6 to 6
- draws: int32 [25600, 12], P(('mol', 'pts')), parts along dimension 0, may hold values from 0 to 3
Outputs:
- new_walkers: bfloat16 [3200, 12, 128], P(('mol', 'pts')), parts along dimension 0
- energy: float32 [48], P('mol'), parts along dimension 0
There are 4 independent parts, one for each index of `mol`. A program takes and returns all parts, laid end to end along the dimension named above; each array names one. Nothing has to cross between parts.
Inputs may be any that keep to these rules, and one draw needn't show every extreme that they name: core is symmetric.
All inputs are finite; a program needn't handle non-finite values.
Results may differ from a plain program's by a relative error of at most 0.018.
Values may be sent and summed in bfloat16 or wider, within the bound.
No kernel may reach another device: no remote copies, remote signals or barrier semaphores. Data moves between devices by JAX's collectives and lax.ppermute only.
A program may use at most 192 MiB of HBM per device.

v0:
```python
import functools
import math

import jax
import jax.numpy as jnp
from jax import lax
from jax.experimental import pallas as pl
from jax.experimental.pallas import tpu as pltpu
from jax.sharding import PartitionSpec as P

TAYLOR = 3
GAUSS_NODES = (-2.3344142, -0.7419637, 0.7419637, 2.3344142)
FIELD_STEP = 0.15
BF16, F32 = jnp.bfloat16, jnp.float32
NT = (((1,), (1,)), ((), ()))
NN = (((1,), (0,)), ((), ()))
VMEM_LIMIT = 24 * 1024 * 1024


def mm(a, b, dims=NN):
    return lax.dot_general(a, b, dims, preferred_element_type=F32)


def node_lookup(draws):
    values = jnp.zeros(draws.shape, F32)
    for number, node in enumerate(GAUSS_NODES):
        values = values + jnp.where(draws == number, node, 0.0).astype(F32)
    return values


def vmem():
    return pl.BlockSpec(memory_space=pltpu.VMEM)


def cost(flops, moved):
    return pl.CostEstimate(flops=int(flops), bytes_accessed=int(moved), transcendentals=0)


def params():
    return pltpu.CompilerParams(vmem_limit_bytes=VMEM_LIMIT)


def anywhere():
    return pl.BlockSpec(memory_space=pl.ANY)


def position():
    me = lax.axis_index("pts")
    chip = lax.div(me, 2)
    return me, chip, me - 2 * chip


def orbit_kernel(occupied, own_ref, mate_ref, w_ref, trial_any, orbit_ref, near_ref, sent_ref, trial_ref, sems):
    me, _, parity = position()
    copies = [
        pltpu.make_async_copy(trial_any.at[device], trial_ref.at[k], sems.at[k])
        for k, device in enumerate((me, me + 1 - 2 * parity))
    ]
    for copy in copies:
        copy.start()
    rows = own_ref.shape[0]
    x = jnp.concatenate([own_ref[...].astype(F32), mate_ref[...].astype(F32)], axis=0).astype(BF16)
    for copy in copies:
        copy.wait()
    trial = trial_ref[0].astype(F32)
    near = jnp.concatenate([trial, trial_ref[1].astype(F32)], axis=0)
    near_ref[...] = near.astype(BF16)
    lane = lax.broadcasted_iota(jnp.int32, (rows, 128), 1)
    density = jnp.zeros((rows, 128), F32)
    for pair in range(w_ref.shape[0] // (2 * occupied)):
        both = mm(x, w_ref[pair * 2 * occupied : (pair + 1) * 2 * occupied], NT).astype(BF16)
        for half in range(2):
            one = both[:, half * occupied : (half + 1) * occupied]
            walker = 2 * pair + half
            orbit_ref[walker] = one
            total = jnp.sum(one.astype(F32)[:rows] * trial, axis=1, keepdims=True)
            density = jnp.where(lane == walker, total / math.sqrt(occupied), density)
    turned = density.T[: sent_ref.shape[1]].astype(BF16)
    for device in range(sent_ref.shape[0]):
        sent_ref[device] = turned


def orbit_call(own, mate, turned_walkers, trial_blocks):
    rows, orbitals = own.shape
    devices, _, occupied = trial_blocks.shape
    walkers = turned_walkers.shape[0] // occupied
    return pl.pallas_call(
        functools.partial(orbit_kernel, occupied),
        out_shape=(
            jax.ShapeDtypeStruct((walkers, 2 * rows, occupied), BF16),
            jax.ShapeDtypeStruct((2 * rows, occupied), BF16),
            jax.ShapeDtypeStruct((devices // 2, -(-walkers // 16) * 16, rows), BF16),
        ),
        in_specs=[vmem()] * 3 + [anywhere()],
        out_specs=(vmem(), vmem(), vmem()),
        scratch_shapes=[pltpu.VMEM((2, rows, occupied), BF16), pltpu.SemaphoreType.DMA((2,))],
        compiler_params=params(),
        cost_estimate=cost(4 * rows * orbitals * walkers * occupied, 6e6),
        name="orbit",
    )(own, mate, turned_walkers, trial_blocks)


def split_kernel(core_ref, out_ref):
    width = out_ref.shape[3]
    _, _, parity = position()
    for block in range(core_ref.shape[1] // width):
        slot = lax.rem(block % 2 + parity, 2)
        out_ref[slot, block // 2] = core_ref[:, block * width : (block + 1) * width]


def split_call(core, width):
    rows, columns = core.shape
    return pl.pallas_call(
        split_kernel,
        out_shape=jax.ShapeDtypeStruct((2, columns // width // 2, rows, width), BF16),
        in_specs=[vmem()],
        out_specs=vmem(),
        compiler_params=params(),
        cost_estimate=cost(1e6, 6e6),
        name="split",
    )(core)


def field_kernel(walkers, occupied, columns, mine_ref, theirs_ref, cores_ref, draws_ref, out_ref, hartree_ref):
    total = None
    for chip in range(cores_ref.shape[1]):
        for slot, density_ref in enumerate((mine_ref, theirs_ref)):
            piece = mm(density_ref[chip], cores_ref[slot, chip], NT)
            total = piece if total is None else total + piece
    mine = mine_ref[position()[1]].astype(F32)
    hartree_ref[...] = jnp.broadcast_to(jnp.sum(mine * total, axis=1, keepdims=True), hartree_ref.shape)
    field = FIELD_STEP * (node_lookup(draws_ref[...]) - FIELD_STEP * total[:walkers])
    for chip in range(out_ref.shape[0]):
        first = columns * chip // occupied
        out_ref[chip, 0:1] = field[first : first + 1]
        second = min(first + 1, walkers - 1)
        out_ref[chip, 1:2] = field[second : second + 1]


def field_call(mine, theirs, cores, draws, occupied, columns):
    chips, padded, rows = mine.shape
    walkers = draws.shape[0]
    return pl.pallas_call(
        functools.partial(field_kernel, walkers, occupied, columns),
        out_shape=(
            jax.ShapeDtypeStruct((chips, 2, rows), F32),
            jax.ShapeDtypeStruct((padded, 128), F32),
        ),
        in_specs=[vmem()] * 4,
        out_specs=(vmem(), vmem()),
        compiler_params=params(),
        cost_estimate=cost(4e9, 4e6),
        name="field",
    )(mine, theirs, cores, draws)


def exchange_kernel(
    occupied, weight, offset, x_ref, w_ref, orbit_ref, near_ref, before_ref, trial_any, cores_any,
    came_any, out_ref, core_ref, far_ref, forward_ref, backward_ref, trial_ref, half_ref, sems,
):
    _, chip, parity = position()
    chips = cores_any.shape[1]
    far = lax.rem(chip + (offset + chips), chips)
    copies = [
        pltpu.make_async_copy(trial_any.at[2 * far + parity], trial_ref, sems.at[0]),
        pltpu.make_async_copy(cores_any.at[0, far], half_ref.at[0], sems.at[1]),
        pltpu.make_async_copy(came_any.at[0, far], half_ref.at[1], sems.at[2]),
    ]
    for copy in copies:
        copy.start()
    x = x_ref[...]
    rows = x.shape[0]
    far_ref[...] = mm(w_ref[...], x, NT).astype(BF16)
    for copy in copies:
        copy.wait()
    core_ref[:rows] = half_ref[0].astype(F32)
    core_ref[rows:] = half_ref[1].astype(F32)
    far_trial = trial_ref[...]
    walkers = out_ref.shape[0]
    forward_ref[1] = jnp.zeros(core_ref.shape, F32)
    backward_ref[1] = jnp.zeros(core_ref.shape, F32)

    def gather(walker, slot):
        value = forward_ref[slot] * backward_ref[slot] * core_ref[...]
        total = jnp.sum(value.reshape(-1, 8, rows), axis=0)
        out_ref[walker] = before_ref[walker] + weight * total

    def spread(walker, slot):
        orbit_far = far_ref[pl.ds(pl.multiple_of(walker * occupied, occupied), occupied)]
        forward_ref[slot] = mm(orbit_ref[walker], far_trial, NT)
        backward_ref[slot] = mm(near_ref[...], orbit_far)

    def two(number, carry):
        gather(lax.rem(2 * number + walkers - 1, walkers), 1)
        spread(2 * number, 0)
        gather(2 * number, 0)
        spread(2 * number + 1, 1)
        return carry

    lax.fori_loop(0, walkers // 2, two, 0)
    gather(walkers - 1, 1)


def exchange_call(offset, block, turned_walkers, orbit, near, trial_blocks, cores, came, before, weight):
    walkers, near_rows, occupied = orbit.shape
    rows = came.shape[2]
    orbitals = turned_walkers.shape[1]
    return pl.pallas_call(
        functools.partial(exchange_kernel, occupied, weight, offset),
        out_shape=jax.ShapeDtypeStruct(before.shape, F32),
        in_specs=[vmem()] * 5 + [anywhere()] * 3,
        out_specs=vmem(),
        scratch_shapes=[
            pltpu.VMEM((near_rows, rows), F32),
            pltpu.VMEM((walkers * occupied, rows), BF16),
            pltpu.VMEM((2, near_rows, rows), F32),
            pltpu.VMEM((2, near_rows, rows), F32),
            pltpu.VMEM((rows, occupied), BF16),
            pltpu.VMEM((2, rows, rows), BF16),
            pltpu.SemaphoreType.DMA((3,)),
        ],
        compiler_params=params(),
        cost_estimate=cost(2 * rows * walkers * occupied * (orbitals + 4 * rows), 5e6),
        name="exchange",
    )(block, turned_walkers, orbit, near, before, trial_blocks, cores, came)


def energy_row(walkers, occupied, shift, partial_ref, hartree_ref, points):
    exchange = jnp.sum(jnp.sum(partial_ref[...], axis=1), axis=1, keepdims=True) / occupied
    energy = (hartree_ref[:walkers] - exchange) / (2.0 * points)
    row = lax.broadcasted_iota(jnp.int32, energy.shape, 0)
    lane = lax.broadcasted_iota(jnp.int32, energy.shape, 1)
    return jnp.sum(jnp.where(lane == row + shift, energy, 0.0), axis=0, keepdims=True)


def step_term(degree, own_ref, other_ref, running_ref):
    columns = running_ref.shape[0]
    term = ((own_ref[:columns] + other_ref[:columns]) / degree).astype(BF16)
    return term, running_ref[...] + term.astype(F32)


def degree_kernel(offsets, degree, occupied, field_ref, *refs):
    count = len(offsets)
    _, chip, _ = position()
    blocks, refs = refs[:count], refs[count:]
    if degree == 1:
        walkers_any, partial_ref, hartree_ref, out_ref, running_ref, walkers_ref, sem = refs
        columns = walkers_ref.shape[0]
        start = pl.multiple_of(chip * columns, math.gcd(columns, 32))
        copy = pltpu.make_async_copy(walkers_any.at[pl.ds(start, columns)], walkers_ref, sem)
        copy.start()
        copy.wait()
        term = walkers_ref[...]
        running_ref[...] = term.astype(F32)
        points = 2 * count * field_ref.shape[2]
        row = energy_row(partial_ref.shape[0], occupied, columns, partial_ref, hartree_ref, points)
        out_ref[columns:, :128] = jnp.broadcast_to(row, (8, 128))
    else:
        own_ref, other_ref, before_ref, out_ref, running_ref = refs
        columns = before_ref.shape[0]
        term, running = step_term(degree - 1, own_ref, other_ref, before_ref)
        running_ref[...] = running
    first = occupied - lax.rem(chip * columns, occupied)
    total = None
    for number in range(count):
        x = blocks[number][...]
        current = mm(term, x, NT).astype(BF16).astype(F32)
        field = field_ref[lax.rem(chip + (offsets[number] + count), count)]
        column = lax.broadcasted_iota(jnp.int32, current.shape, 0)
        scaled = jnp.where(column < first, field[0:1], field[1:2]) * current
        piece = mm(scaled.astype(BF16), x)
        total = piece if total is None else total + piece
    out_ref[:columns] = total


def degree_call(offsets, fields, blocks, degree, occupied, columns, *rest):
    count = len(blocks)
    rows, orbitals = fields.shape[2], blocks[0].shape[1]
    return pl.pallas_call(
        functools.partial(degree_kernel, tuple(offsets), degree, occupied),
        out_shape=(
            jax.ShapeDtypeStruct((columns + 8 if degree == 1 else columns, orbitals), F32),
            jax.ShapeDtypeStruct((columns, orbitals), F32),
        ),
        in_specs=[vmem()] * (1 + count)
        + [anywhere() if degree == 1 else vmem()]
        + [vmem()] * (len(rest) - 1),
        out_specs=(vmem(), vmem()),
        scratch_shapes=[pltpu.VMEM((columns, orbitals), BF16), pltpu.SemaphoreType.DMA(())]
        if degree == 1
        else [],
        compiler_params=params(),
        cost_estimate=cost(4 * rows * count * orbitals * columns, 6e6),
        name="degree",
    )(fields, *blocks, *rest)


def finish_kernel(own_ref, other_ref, before_ref, own_energy, other_energy, out_ref, turned_ref):
    columns, orbitals = before_ref.shape
    chips, own_rows, lanes = out_ref.shape
    _, _, parity = position()
    _, running = step_term(TAYLOR, own_ref, other_ref, before_ref)
    padded = jnp.concatenate([running, jnp.zeros((lanes - columns, orbitals), F32)], axis=0)
    turned_ref[...] = padded.T
    energy = own_energy[:, :lanes] + other_energy[:, :lanes]
    top = energy.astype(BF16).astype(F32)
    middle = (energy - top).astype(BF16).astype(F32)
    low = energy - top - middle
    row = lax.broadcasted_iota(jnp.int32, (own_rows, lanes), 0)
    lane = lax.broadcasted_iota(jnp.int32, (own_rows, lanes), 1)
    extra = jnp.where(row == 0, top[0:1], jnp.where(row == 1, middle[0:1], jnp.where(row == 2, low[0:1], 0.0)))
    for chip in range(chips):
        mine = turned_ref[pl.ds((2 * chip + parity) * own_rows, own_rows)]
        out_ref[chip] = jnp.where(lane < columns, mine, extra).astype(BF16)


def finish_call(own, other, running, own_energy, other_energy, devices):
    columns, orbitals = running.shape
    return pl.pallas_call(
        finish_kernel,
        out_shape=jax.ShapeDtypeStruct((devices // 2, orbitals // devices, 128), BF16),
        in_specs=[vmem()] * 5,
        out_specs=vmem(),
        scratch_shapes=[pltpu.VMEM((orbitals, 128), F32)],
        compiler_params=params(),
        cost_estimate=cost(1e6, 2e6),
        name="finish",
    )(own, other, running, own_energy, other_energy)


def body(points_map, trial, core, walkers, draws):
    rows, orbitals = points_map.shape
    walker_count, occupied = walkers.shape[1:]
    devices = lax.axis_size("pts")
    chips = devices // 2
    swapped = [(i, i ^ 1) for i in range(devices)]
    forward = [(i, (i + 2) % devices) for i in range(devices)]
    backward = [(i, (i - 2) % devices) for i in range(devices)]
    same_core = [[2 * z + c for z in range(chips)] for c in range(2)]
    columns = walker_count * occupied // chips

    def swap(value):
        return lax.ppermute(value, "pts", swapped)

    mate = swap(points_map)
    turned = walkers.reshape(orbitals, walker_count * occupied).T
    trial_blocks = trial.reshape(devices, rows, occupied)
    orbit, near, sent = orbit_call(points_map, mate, turned, trial_blocks)
    mine = lax.all_to_all(
        sent, "pts", split_axis=0, concat_axis=0, tiled=True, axis_index_groups=same_core
    )
    theirs = swap(mine)
    cores = split_call(core, rows)
    came = swap(cores[1:2])
    outgoing, hartree = field_call(mine, theirs, cores, draws.T, occupied, columns)
    fields = lax.all_to_all(
        outgoing, "pts", split_axis=0, concat_axis=0, tiled=True, axis_index_groups=same_core
    )

    def exchange(offset, block, before, weight):
        return exchange_call(
            offset, block, turned, orbit, near, trial_blocks, cores, came, before, weight
        )

    partial = jnp.zeros((walker_count, 8, rows), F32)
    partial, fields = lax.optimization_barrier((partial, fields))
    half = chips // 2
    right = left = points_map
    blocks, offsets = [points_map], [0]
    for step in range(half):
        if step > 1:
            right, partial = lax.optimization_barrier((right, partial))
        after = lax.ppermute(right, "pts", forward)
        partial = exchange(-step, right, partial, 2.0 if step else 1.0)
        if step > 1:
            left, partial = lax.optimization_barrier((left, partial))
        if step < half - 1:
            left = lax.ppermute(left, "pts", backward)
            blocks.append(left)
            offsets.append(step + 1)
        right = after
        blocks.append(right)
        offsets.append(-step - 1)
    partial = exchange(-half, right, partial, 1.0)

    mine, running = degree_call(
        offsets, fields, blocks, 1, occupied, columns, turned, partial, hartree
    )
    theirs = swap(mine)
    energies = (mine[columns:], theirs[columns:])
    for degree in range(2, TAYLOR + 1):
        mine, running = degree_call(
            offsets, fields, blocks, degree, occupied, columns, mine, theirs, running
        )
        theirs = swap(mine)
    message = finish_call(mine, theirs, running, *energies, devices)
    arrived = lax.all_to_all(
        message, "pts", split_axis=0, concat_axis=0, tiled=True, axis_index_groups=same_core
    )
    new_walkers = jnp.moveaxis(arrived[:, :, :columns], 0, 1)
    new_walkers = new_walkers.reshape(orbitals // devices, walker_count, occupied)
    energy = jnp.sum(arrived[:, :3, columns : columns + walker_count].astype(F32), axis=(0, 1))
    return (new_walkers, energy)


def solution(mesh):
    placed = (
        P(("mol", "pts"), None),
        P("mol", None),
        P(("mol", "pts"), None),
        P("mol", None, None),
        P(("mol", "pts"), None),
    )
    return jax.shard_map(
        body,
        mesh=mesh,
        in_specs=placed,
        out_specs=(P(("mol", "pts"), None, None), P("mol")),
        check_vma=False,
    )
```

profile of v0, /device:TPU:70, one launch (start us, length us, event | category | flops | bytes accessed | tf_op | source)
XLA Modules:
  0.0 201.9 jit_solution(10280195255691481960)
XLA Ops:
  0.8 1.7 copy-done.9
  2.5 1.3 split.1.cores_ref.cores_any
  3.8 1.4 slice.20
  6.4 3.2 %copy.8 = bf16[800,12,128]{0,2,1:T(8,128)(2,1)S(1)} copy(bf16[800,12,128]{2,0,1:T(8,128)(2,1)} %param.8) | data formatting | bytes 4915200 | tf_op args[3]
  10.4 1.4 copy-done.4
  11.8 1.0 copy-done.11
  12.8 2.4 %orbit.1 = (bf16[12,400,128]{2,1,0:T(8,128)(2,1)S(1)}, bf16[400,128]{1,0:T(8,128)(2,1)S(1)}, bf16[16,16,200]{2,1,0:T(8,128)(2,1)}) custom-call(bf16[200,800]{1,0:T(8,128)(2,1)S(1)} %copy-done.8, bf16[200,800]{1,0:T(8,128)(2,1)S(1)} %copy-done.11, bf16[1536,800]{1,0:T(8,128)(2,1)S(1)} %bitcast.7, bf16[32,200,128]{2,1,0:T(8,128)(2,1)S(1)} %bitcast.18), custom_call_target="tpu_custom_call" | custom-call | flops 983040000 | bytes 6000000 | tf_op jit(solution)/shard_map/orbit/pallas_call | solution.py:87
  15.3 1.0 copy-done.6
  16.3 17.0 %all-to-all-start = ((bf16[16,16,200]{2,1,0:T(8,128)(2,1)}), bf16[16,16,200]{2,1,0:T(8,128)(2,1)S(1)}, u32[]{:S(2)}, u32[]{:S(2)}) async-start(bf16[16,16,200]{2,1,0:T(8,128)(2,1)} %get-tuple-element.38), calls=%async_computation | async-start | bytes 262144 | tf_op jit(solution)/shard_map/all_to_all | solution.py:349
  33.3 1.7 collective-permute-start.3
  35.1 14.2 %all-to-all-done.mine_ref = bf16[16,16,200]{2,1,0:T(8,128)(2,1)S(1)} async-done(((bf16[16,16,200]{2,1,0:T(8,128)(2,1)}), bf16[16,16,200]{2,1,0:T(8,128)(2,1)S(1)}, u32[]{:S(2)}, u32[]{:S(2)}) %all-to-all-start) | async-done | bytes 102432 | tf_op jit(solution)/shard_map/all_to_all | solution.py:349
  49.3 1.4 collective-permute-start.2
  51.4 1.9 copy-done.1
  53.3 1.6 field.1
  54.9 10.0 %all-to-all-start.1 = ((f32[16,2,200]{2,1,0:T(2,128)}), f32[16,2,200]{2,1,0:T(2,128)S(1)}, u32[]{:S(2)}, u32[]{:S(2)}) async-start(f32[16,2,200]{2,1,0:T(2,128)} %get-tuple-element.39), calls=%async_computation.1 | async-start | bytes 65536 | tf_op jit(solution)/shard_map/all_to_all | solution.py:356
  64.9 3.0 %collective-permute-start.4 = (bf16[200,800]{1,0:T(8,128)(2,1)}, bf16[200,800]{1,0:T(8,128)(2,1)}, u32[]{:S(2)}, u32[]{:S(2)}) collective-permute-start(bf16[200,800]{1,0:T(8,128)(2,1)} %collective-permute-done.2.refs_1_), channel_id=1, source_target_pairs={{0,30},{1,31},{2,0},{3,1},{4,2},{5,3},{6,4},{7,5},{8,6},{9,7},{10,... | collective-permute-start | bytes 960008 | tf_op jit(solution)/shard_map/ppermute | solution.py:378
  68.0 9.4 %all-to-all-done.1.field_ref = f32[16,2,200]{2,1,0:T(2,128)S(1)} async-done(((f32[16,2,200]{2,1,0:T(2,128)}), f32[16,2,200]{2,1,0:T(2,128)S(1)}, u32[]{:S(2)}, u32[]{:S(2)}) %all-to-all-start.1) | async-done | bytes 25632 | tf_op jit(solution)/shard_map/all_to_all | solution.py:356
  77.4 1.9 copy-done.2
  79.3 1.4 copy-done.5
  80.7 1.3 copy-done.7
  82.0 4.5 %exchange.9.before_ref = f32[12,8,200]{2,1,0:T(8,128)S(1)} custom-call(bf16[200,800]{1,0:T(8,128)(2,1)S(1)} %copy-done.8, bf16[1536,800]{1,0:T(8,128)(2,1)S(1)} %bitcast.8, bf16[12,400,128]{2,1,0:T(8,128)(2,1)S(1)} %copy-done.7, bf16[400,128]{1,0:T(8,128)(2,1)S(1)} %get-tuple-element.42.near_ref, f32[12,8,200]{2,1,0:T(8,128)S(1)} %broadcast_in_dim.3.before_ref, ...), custom_call_target="tpu_custom_call" | custom-call | flops 983040000 | bytes 5000000 | tf_op jit(solution)/shard_map/exchange/pallas_call | solution.py:208
  86.5 5.4 %exchange.10.before_ref = f32[12,8,200]{2,1,0:T(8,128)S(1)} custom-call(bf16[200,800]{1,0:T(8,128)(2,1)} %collective-permute-done.3.x_ref.refs_2_, bf16[1536,800]{1,0:T(8,128)(2,1)S(1)} %bitcast.9, bf16[12,400,128]{2,1,0:T(8,128)(2,1)S(1)} %copy-done.7, bf16[400,128]{1,0:T(8,128)(2,1)S(1)} %get-tuple-element.42.near_ref, ...), custom_call_target="tpu_custom_call" | custom-call | flops 983040000 | bytes 5000000 | tf_op jit(solution)/shard_map/exchange/pallas_call | solution.py:208
  91.9 1.0 collective-permute-start.8
  92.9 5.5 %exchange.11.before_ref = f32[12,8,200]{2,1,0:T(8,128)S(1)} custom-call(bf16[200,800]{1,0:T(8,128)(2,1)} %collective-permute-done.5.x_ref.refs_4_, bf16[1536,800]{1,0:T(8,128)(2,1)S(1)} %bitcast.10, bf16[12,400,128]{2,1,0:T(8,128)(2,1)S(1)} %copy-done.7, bf16[400,128]{1,0:T(8,128)(2,1)S(1)} %get-tuple-element.42.near_ref, ...), custom_call_target="tpu_custom_call" | custom-call | flops 983040000 | bytes 5000000 | tf_op jit(solution)/shard_map/exchange/pallas_call | solution.py:208
  98.4 2.5 %collective-permute-start.7 = (bf16[200,800]{1,0:T(8,128)(2,1)}, bf16[200,800]{1,0:T(8,128)(2,1)S(1)}, u32[]{:S(2)}, u32[]{:S(2)}) collective-permute-start(bf16[200,800]{1,0:T(8,128)(2,1)} %collective-permute-done.4.refs_3_), channel_id=1, source_target_pairs={{0,30},{1,31},{2,0},{3,1},{4,2},{5,3},{6,4},{7,5},{8,6},{9,7},{10,... | collective-permute-start | bytes 960008 | tf_op jit(solution)/shard_map/ppermute | solution.py:378
  100.9 1.0 collective-permute-done.8.x_ref.refs_6_
  101.9 4.5 %exchange.12.before_ref = f32[12,8,200]{2,1,0:T(8,128)S(1)} custom-call(bf16[200,800]{1,0:T(8,128)(2,1)S(1)} %collective-permute-done.8.x_ref.refs_6_, bf16[1536,800]{1,0:T(8,128)(2,1)S(1)} %bitcast.11, bf16[12,400,128]{2,1,0:T(8,128)(2,1)S(1)} %copy-done.7, bf16[400,128]{1,0:T(8,128)(2,1)S(1)} %get-tuple-element.42.near_ref, ...), custom_call_target="tpu_custom_call" | custom-call | flops 983040000 | bytes 5000000 | tf_op jit(solution)/shard_map/exchange/pallas_call | solution.py:208
  107.0 3.5 %collective-permute-start.9 = (bf16[200,800]{1,0:T(8,128)(2,1)S(1)}, bf16[200,800]{1,0:T(8,128)(2,1)S(1)}, u32[]{:S(2)}, u32[]{:S(2)}) collective-permute-start(bf16[200,800]{1,0:T(8,128)(2,1)S(1)} %collective-permute-done.7.refs_5_), channel_id=1, source_target_pairs={{0,30},{1,31},{2,0},{3,1},{4,2},{5,3},{6,4},{7,5},{8,6},{9,7},{10,... | collective-permute-start | bytes 960008 | tf_op jit(solution)/shard_map/ppermute | solution.py:378
  110.6 4.5 %exchange.13.before_ref = f32[12,8,200]{2,1,0:T(8,128)S(1)} custom-call(bf16[200,800]{1,0:T(8,128)(2,1)S(1)} %collective-permute-done.10.x_ref.refs_8_, bf16[1536,800]{1,0:T(8,128)(2,1)S(1)} %bitcast.12, bf16[12,400,128]{2,1,0:T(8,128)(2,1)S(1)} %copy-done.7, bf16[400,128]{1,0:T(8,128)(2,1)S(1)} %get-tuple-element.42.near_ref, ...), custom_call_target="tpu_custom_call" | custom-call | flops 983040000 | bytes 5000000 | tf_op jit(solution)/shard_map/exchange/pallas_call | solution.py:208
  115.7 3.7 %collective-permute-start.11 = (bf16[200,800]{1,0:T(8,128)(2,1)S(1)}, bf16[200,800]{1,0:T(8,128)(2,1)S(1)}, u32[]{:S(2)}, u32[]{:S(2)}) collective-permute-start(bf16[200,800]{1,0:T(8,128)(2,1)S(1)} %collective-permute-done.9.refs_7_), channel_id=1, source_target_pairs={{0,30},{1,31},{2,0},{3,1},{4,2},{5,3},{6,4},{7,5},{8,6},{9,7},{10,... | collective-permute-start | bytes 960008 | tf_op jit(solution)/shard_map/ppermute | solution.py:378
  120.0 4.5 %exchange.14.before_ref = f32[12,8,200]{2,1,0:T(8,128)S(1)} custom-call(bf16[200,800]{1,0:T(8,128)(2,1)S(1)} %collective-permute-done.12.x_ref.refs_10_, bf16[1536,800]{1,0:T(8,128)(2,1)S(1)} %bitcast.13, bf16[12,400,128]{2,1,0:T(8,128)(2,1)S(1)} %copy-done.7, bf16[400,128]{1,0:T(8,128)(2,1)S(1)} %get-tuple-element.42.near_ref, ...), custom_call_target="tpu_custom_call" | custom-call | flops 983040000 | bytes 5000000 | tf_op jit(solution)/shard_map/exchange/pallas_call | solution.py:208
  124.5 1.3 collective-permute-done.11.refs_9_
  125.8 3.7 %collective-permute-start.13 = (bf16[200,800]{1,0:T(8,128)(2,1)S(1)}, bf16[200,800]{1,0:T(8,128)(2,1)S(1)}, u32[]{:S(2)}, u32[]{:S(2)}) collective-permute-start(bf16[200,800]{1,0:T(8,128)(2,1)S(1)} %collective-permute-done.11.refs_9_), channel_id=1, source_target_pairs={{0,30},{1,31},{2,0},{3,1},{4,2},{5,3},{6,4},{7,5},{8,6},{9,7},{10,... | collective-permute-start | bytes 960008 | tf_op jit(solution)/shard_map/ppermute | solution.py:378
  129.5 1.1 collective-permute-done.14.x_ref.refs_12_
  130.6 4.5 %exchange.15.before_ref = f32[12,8,200]{2,1,0:T(8,128)S(1)} custom-call(bf16[200,800]{1,0:T(8,128)(2,1)S(1)} %collective-permute-done.14.x_ref.refs_12_, bf16[1536,800]{1,0:T(8,128)(2,1)S(1)} %bitcast.14, bf16[12,400,128]{2,1,0:T(8,128)(2,1)S(1)} %copy-done.7, bf16[400,128]{1,0:T(8,128)(2,1)S(1)} %get-tuple-element.42.near_ref, ...), custom_call_target="tpu_custom_call" | custom-call | flops 983040000 | bytes 5000000 | tf_op jit(solution)/shard_map/exchange/pallas_call | solution.py:208
  135.1 2.0 collective-permute-done.13.refs_11_
  137.1 3.7 %collective-permute-start.15 = (bf16[200,800]{1,0:T(8,128)(2,1)S(1)}, bf16[200,800]{1,0:T(8,128)(2,1)S(1)}, u32[]{:S(2)}, u32[]{:S(2)}) collective-permute-start(bf16[200,800]{1,0:T(8,128)(2,1)S(1)} %collective-permute-done.13.refs_11_), channel_id=1, source_target_pairs={{0,30},{1,31},{2,0},{3,1},{4,2},{5,3},{6,4},{7,5},{8,6},{9,7},{10,... | collective-permute-start | bytes 960008 | tf_op jit(solution)/shard_map/ppermute | solution.py:378
  140.8 1.6 collective-permute-done.16.x_ref.refs_14_
  142.4 4.5 %exchange.16.before_ref = f32[12,8,200]{2,1,0:T(8,128)S(1)} custom-call(bf16[200,800]{1,0:T(8,128)(2,1)S(1)} %collective-permute-done.16.x_ref.refs_14_, bf16[1536,800]{1,0:T(8,128)(2,1)S(1)} %bitcast.15, bf16[12,400,128]{2,1,0:T(8,128)(2,1)S(1)} %copy-done.7, bf16[400,128]{1,0:T(8,128)(2,1)S(1)} %get-tuple-element.42.near_ref, ...), custom_call_target="tpu_custom_call" | custom-call | flops 983040000 | bytes 5000000 | tf_op jit(solution)/shard_map/exchange/pallas_call | solution.py:208
  146.9 4.1 %collective-permute-done.17.x_ref.refs_15_ = bf16[200,800]{1,0:T(8,128)(2,1)S(1)} collective-permute-done((bf16[200,800]{1,0:T(8,128)(2,1)S(1)}, bf16[200,800]{1,0:T(8,128)(2,1)S(1)}, u32[]{:S(2)}, u32[]{:S(2)}) %collective-permute-start.17) | collective-permute-done | bytes 320032 | tf_op jit(solution)/shard_map/ppermute | solution.py:373
  151.0 4.5 %exchange.17.refs_17_ = f32[12,8,200]{2,1,0:T(8,128)S(1)} custom-call(bf16[200,800]{1,0:T(8,128)(2,1)S(1)} %collective-permute-done.17.x_ref.refs_15_, bf16[1536,800]{1,0:T(8,128)(2,1)S(1)} %bitcast.16, bf16[12,400,128]{2,1,0:T(8,128)(2,1)S(1)} %copy-done.7, bf16[400,128]{1,0:T(8,128)(2,1)S(1)} %get-tuple-element.42.near_ref, ...), custom_call_target="tpu_custom_call" | custom-call | flops 983040000 | bytes 5000000 | tf_op jit(solution)/shard_map/exchange/pallas_call | solution.py:208
  155.4 7.7 %degree.3 = (f32[104,800]{1,0:T(8,128)S(1)}, f32[96,800]{1,0:T(8,128)S(1)}) custom-call(f32[16,2,200]{2,1,0:T(2,128)S(1)} %all-to-all-done.1.field_ref, bf16[200,800]{1,0:T(8,128)(2,1)S(1)} %copy-done.8, bf16[200,800]{1,0:T(8,128)(2,1)} %collective-permute-done.2.refs_1_, bf16[200,800]{1,0:T(8,128)(2,1)} %collective-permute-done.3.x_ref.refs_2_, ...), custom_call_target="tpu_custom_call" | custom-call | flops 983040000 | bytes 6000000 | tf_op jit(solution)/shard_map/degree/pallas_call | solution.py:279
  163.3 1.7 collective-permute-done.18.refs_17_
  165.0 7.5 %degree.4 = (f32[96,800]{1,0:T(8,128)S(1)}, f32[96,800]{1,0:T(8,128)S(1)}) custom-call(f32[16,2,200]{2,1,0:T(2,128)S(1)} %all-to-all-done.1.field_ref, bf16[200,800]{1,0:T(8,128)(2,1)S(1)} %copy-done.8, bf16[200,800]{1,0:T(8,128)(2,1)} %collective-permute-done.2.refs_1_, bf16[200,800]{1,0:T(8,128)(2,1)} %collective-permute-done.3.x_ref.refs_2_, ...), custom_call_target="tpu_custom_call" | custom-call | flops 983040000 | bytes 6000000 | tf_op jit(solution)/shard_map/degree/pallas_call | solution.py:279
  172.8 1.5 collective-permute-done.19.refs_17_
  174.3 7.5 %degree.5 = (f32[96,800]{1,0:T(8,128)S(1)}, f32[96,800]{1,0:T(8,128)S(1)}) custom-call(f32[16,2,200]{2,1,0:T(2,128)S(1)} %all-to-all-done.1.field_ref, bf16[200,800]{1,0:T(8,128)(2,1)S(1)} %copy-done.8, bf16[200,800]{1,0:T(8,128)(2,1)} %collective-permute-done.2.refs_1_, bf16[200,800]{1,0:T(8,128)(2,1)} %collective-permute-done.3.x_ref.refs_2_, ...), custom_call_target="tpu_custom_call" | custom-call | flops 983040000 | bytes 6000000 | tf_op jit(solution)/shard_map/degree/pallas_call | solution.py:279
  182.1 1.5 collective-permute-done.20.other_ref
  183.8 16.6 %all_to_all.15 = bf16[16,25,128]{2,1,0:T(8,128)(2,1)S(1)} all-to-all(bf16[16,25,128]{2,1,0:T(8,128)(2,1)S(1)} %finish.1), channel_id=1, replica_groups={{0,2,4,6,8,10,12,14,16,18,20,22,24,26,28,30},{1,3,5,7,9,11,13,15,17,19,..., dimensions={0} | all-to-all | bytes 204800 | tf_op jit(solution)/shard_map/all_to_all | solution.py:397
  (51 shorter events, 7.1 us)
Async XLA Ops:
  0.6 9.0 %collective-permute-start = (bf16[200,800]{1,0:T(8,128)(2,1)}, bf16[200,800]{1,0:T(8,128)(2,1)S(1)}, u32[]{:S(2)}, u32[]{:S(2)}) collective-permute-start(bf16[200,800]{1,0:T(8,128)(2,1)} %refs_0_.5), channel_id=1, source_target_pairs={{0,1},{1,0},{2,3},{3,2},{4,5},{5,4},{6,7},{7,6},{8,9},{9,8},{10,11... | collective-permute-start | bytes 960008 | tf_op jit(solution)/shard_map/ppermute | solution.py:343
  0.8 1.7 copy-start.9
  3.8 2.2 %copy-start = (bf16[2,16,200,200]{3,2,1,0:T(8,128)(2,1)}, bf16[2,16,200,200]{3,2,1,0:T(8,128)(2,1)S(1)}, u32[]{:S(2)}) copy-start(bf16[2,16,200,200]{3,2,1,0:T(8,128)(2,1)S(1)} %split.1.cores_ref.cores_any) | copy-start | bytes 7680004
  5.9 4.5 %copy-start.8 = (bf16[200,800]{1,0:T(8,128)(2,1)S(1)}, bf16[200,800]{1,0:T(8,128)(2,1)}, u32[]{:S(2)}) copy-start(bf16[200,800]{1,0:T(8,128)(2,1)} %refs_0_.5) | copy-start | bytes 960004
  5.9 71.4 %collective-permute-start.6 = (bf16[1,16,200,200]{3,2,1,0:T(8,128)(2,1)}, bf16[1,16,200,200]{3,2,1,0:T(8,128)(2,1)}, u32[]{:S(2)}, u32[]{:S(2)}) collective-permute-start(bf16[1,16,200,200]{3,2,1,0:T(8,128)(2,1)} %slice.20), channel_id=1, source_target_pairs={{0,1},{1,0},{2,3},{3,2},{4,5},{5,4},{6,7},{7,6},{8,9},{9,8},{10,11... | collective-permute-start | bytes 3840008 | tf_op jit(solution)/shard_map/ppermute | solution.py:343
  9.7 0.7 copy-start.10
  10.4 1.4 copy-start.4
  11.8 1.0 copy-start.11
  12.8 38.5 %copy-start.12 = (s32[200,12]{0,1:T(8,128)S(1)}, s32[200,12]{0,1:T(8,128)}, u32[]{:S(2)}) copy-start(s32[200,12]{0,1:T(8,128)} %param.9) | copy-start | bytes 28804
  15.3 1.1 copy-start.6
  16.3 33.0 %all-to-all-start = ((bf16[16,16,200]{2,1,0:T(8,128)(2,1)}), bf16[16,16,200]{2,1,0:T(8,128)(2,1)S(1)}, u32[]{:S(2)}, u32[]{:S(2)}) async-start(bf16[16,16,200]{2,1,0:T(8,128)(2,1)} %get-tuple-element.38), calls=%async_computation | async-start | bytes 262144 | tf_op jit(solution)/shard_map/all_to_all | solution.py:349
  33.3 17.4 %collective-permute-start.3 = (bf16[200,800]{1,0:T(8,128)(2,1)S(1)}, bf16[200,800]{1,0:T(8,128)(2,1)}, u32[]{:S(2)}, u32[]{:S(2)}) collective-permute-start(bf16[200,800]{1,0:T(8,128)(2,1)S(1)} %copy-done.8), channel_id=1, source_target_pairs={{0,2},{1,3},{2,4},{3,5},{4,6},{5,7},{6,8},{7,9},{8,10},{9,11},{10,... | collective-permute-start | bytes 960008 | tf_op jit(solution)/shard_map/ppermute | solution.py:373
  49.3 2.0 %collective-permute-start.1 = (bf16[16,16,200]{2,1,0:T(8,128)(2,1)S(1)}, bf16[16,16,200]{2,1,0:T(8,128)(2,1)S(1)}, u32[]{:S(2)}, u32[]{:S(2)}) collective-permute-start(bf16[16,16,200]{2,1,0:T(8,128)(2,1)S(1)} %all-to-all-done.mine_ref), channel_id=1, source_target_pairs={{0,1},{1,0},{2,3},{3,2},{4,5},{5,4},{6,7},{7,6},{8,9},{9,8},{10,11... | collective-permute-start | bytes 307208 | tf_op jit(solution)/shard_map/ppermute | solution.py:343
  49.3 15.6 %collective-permute-start.2 = (bf16[200,800]{1,0:T(8,128)(2,1)S(1)}, bf16[200,800]{1,0:T(8,128)(2,1)}, u32[]{:S(2)}, u32[]{:S(2)}) collective-permute-start(bf16[200,800]{1,0:T(8,128)(2,1)S(1)} %copy-done.8), channel_id=1, source_target_pairs={{0,30},{1,31},{2,0},{3,1},{4,2},{5,3},{6,4},{7,5},{8,6},{9,7},{10,... | collective-permute-start | bytes 960008 | tf_op jit(solution)/shard_map/ppermute | solution.py:378
  50.7 41.2 %collective-permute-start.5 = (bf16[200,800]{1,0:T(8,128)(2,1)}, bf16[200,800]{1,0:T(8,128)(2,1)}, u32[]{:S(2)}, u32[]{:S(2)}) collective-permute-start(bf16[200,800]{1,0:T(8,128)(2,1)} %collective-permute-done.3.x_ref.refs_2_), channel_id=1, source_target_pairs={{0,2},{1,3},{2,4},{3,5},{4,6},{5,7},{6,8},{7,9},{8,10},{9,11},{10,... | collective-permute-start | bytes 960008 | tf_op jit(solution)/shard_map/ppermute | solution.py:373
  51.3 1.9 copy-start.1
  54.9 22.4 %all-to-all-start.1 = ((f32[16,2,200]{2,1,0:T(2,128)}), f32[16,2,200]{2,1,0:T(2,128)S(1)}, u32[]{:S(2)}, u32[]{:S(2)}) async-start(f32[16,2,200]{2,1,0:T(2,128)} %get-tuple-element.39), calls=%async_computation.1 | async-start | bytes 65536 | tf_op jit(solution)/shard_map/all_to_all | solution.py:356
  64.9 33.4 %collective-permute-start.4 = (bf16[200,800]{1,0:T(8,128)(2,1)}, bf16[200,800]{1,0:T(8,128)(2,1)}, u32[]{:S(2)}, u32[]{:S(2)}) collective-permute-start(bf16[200,800]{1,0:T(8,128)(2,1)} %collective-permute-done.2.refs_1_), channel_id=1, source_target_pairs={{0,30},{1,31},{2,0},{3,1},{4,2},{5,3},{6,4},{7,5},{8,6},{9,7},{10,... | collective-permute-start | bytes 960008 | tf_op jit(solution)/shard_map/ppermute | solution.py:378
  77.4 1.9 copy-start.2
  79.3 1.4 copy-start.5
  80.7 1.3 copy-start.7
  82.0 4.5 %copy-start.3 = (bf16[2,16,200,200]{3,2,1,0:T(8,128)(2,1)S(1)}, bf16[2,16,200,200]{3,2,1,0:T(8,128)(2,1)}, u32[]{:S(2)}) copy-start(bf16[2,16,200,200]{3,2,1,0:T(8,128)(2,1)} %copy-done) | copy-start | bytes 7680004
  91.9 9.9 %collective-permute-start.8 = (bf16[200,800]{1,0:T(8,128)(2,1)}, bf16[200,800]{1,0:T(8,128)(2,1)S(1)}, u32[]{:S(2)}, u32[]{:S(2)}) collective-permute-start(bf16[200,800]{1,0:T(8,128)(2,1)} %collective-permute-done.5.x_ref.refs_4_), channel_id=1, source_target_pairs={{0,2},{1,3},{2,4},{3,5},{4,6},{5,7},{6,8},{7,9},{8,10},{9,11},{10,... | collective-permute-start | bytes 960008 | tf_op jit(solution)/shard_map/ppermute | solution.py:373
  98.4 8.6 %collective-permute-start.7 = (bf16[200,800]{1,0:T(8,128)(2,1)}, bf16[200,800]{1,0:T(8,128)(2,1)S(1)}, u32[]{:S(2)}, u32[]{:S(2)}) collective-permute-start(bf16[200,800]{1,0:T(8,128)(2,1)} %collective-permute-done.4.refs_3_), channel_id=1, source_target_pairs={{0,30},{1,31},{2,0},{3,1},{4,2},{5,3},{6,4},{7,5},{8,6},{9,7},{10,... | collective-permute-start | bytes 960008 | tf_op jit(solution)/shard_map/ppermute | solution.py:378
  101.9 8.7 %collective-permute-start.10 = (bf16[200,800]{1,0:T(8,128)(2,1)S(1)}, bf16[200,800]{1,0:T(8,128)(2,1)S(1)}, u32[]{:S(2)}, u32[]{:S(2)}) collective-permute-start(bf16[200,800]{1,0:T(8,128)(2,1)S(1)} %collective-permute-done.8.x_ref.refs_6_), channel_id=1, source_target_pairs={{0,2},{1,3},{2,4},{3,5},{4,6},{5,7},{6,8},{7,9},{8,10},{9,11},{10,... | collective-permute-start | bytes 960008 | tf_op jit(solution)/shard_map/ppermute | solution.py:373
  107.0 8.7 %collective-permute-start.9 = (bf16[200,800]{1,0:T(8,128)(2,1)S(1)}, bf16[200,800]{1,0:T(8,128)(2,1)S(1)}, u32[]{:S(2)}, u32[]{:S(2)}) collective-permute-start(bf16[200,800]{1,0:T(8,128)(2,1)S(1)} %collective-permute-done.7.refs_5_), channel_id=1, source_target_pairs={{0,30},{1,31},{2,0},{3,1},{4,2},{5,3},{6,4},{7,5},{8,6},{9,7},{10,... | collective-permute-start | bytes 960008 | tf_op jit(solution)/shard_map/ppermute | solution.py:378
  110.6 9.4 %collective-permute-start.12 = (bf16[200,800]{1,0:T(8,128)(2,1)S(1)}, bf16[200,800]{1,0:T(8,128)(2,1)S(1)}, u32[]{:S(2)}, u32[]{:S(2)}) collective-permute-start(bf16[200,800]{1,0:T(8,128)(2,1)S(1)} %collective-permute-done.10.x_ref.refs_8_), channel_id=1, source_target_pairs={{0,2},{1,3},{2,4},{3,5},{4,6},{5,7},{6,8},{7,9},{8,10},{9,11},{10,... | collective-permute-start | bytes 960008 | tf_op jit(solution)/shard_map/ppermute | solution.py:373
  115.7 10.1 %collective-permute-start.11 = (bf16[200,800]{1,0:T(8,128)(2,1)S(1)}, bf16[200,800]{1,0:T(8,128)(2,1)S(1)}, u32[]{:S(2)}, u32[]{:S(2)}) collective-permute-start(bf16[200,800]{1,0:T(8,128)(2,1)S(1)} %collective-permute-done.9.refs_7_), channel_id=1, source_target_pairs={{0,30},{1,31},{2,0},{3,1},{4,2},{5,3},{6,4},{7,5},{8,6},{9,7},{10,... | collective-permute-start | bytes 960008 | tf_op jit(solution)/shard_map/ppermute | solution.py:378
  120.0 10.6 %collective-permute-start.14 = (bf16[200,800]{1,0:T(8,128)(2,1)S(1)}, bf16[200,800]{1,0:T(8,128)(2,1)S(1)}, u32[]{:S(2)}, u32[]{:S(2)}) collective-permute-start(bf16[200,800]{1,0:T(8,128)(2,1)S(1)} %collective-permute-done.12.x_ref.refs_10_), channel_id=1, source_target_pairs={{0,2},{1,3},{2,4},{3,5},{4,6},{5,7},{6,8},{7,9},{8,10},{9,11},{10,... | collective-permute-start | bytes 960008 | tf_op jit(solution)/shard_map/ppermute | solution.py:373
  125.8 11.3 %collective-permute-start.13 = (bf16[200,800]{1,0:T(8,128)(2,1)S(1)}, bf16[200,800]{1,0:T(8,128)(2,1)S(1)}, u32[]{:S(2)}, u32[]{:S(2)}) collective-permute-start(bf16[200,800]{1,0:T(8,128)(2,1)S(1)} %collective-permute-done.11.refs_9_), channel_id=1, source_target_pairs={{0,30},{1,31},{2,0},{3,1},{4,2},{5,3},{6,4},{7,5},{8,6},{9,7},{10,... | collective-permute-start | bytes 960008 | tf_op jit(solution)/shard_map/ppermute | solution.py:378
  130.6 11.7 %collective-permute-start.16 = (bf16[200,800]{1,0:T(8,128)(2,1)S(1)}, bf16[200,800]{1,0:T(8,128)(2,1)S(1)}, u32[]{:S(2)}, u32[]{:S(2)}) collective-permute-start(bf16[200,800]{1,0:T(8,128)(2,1)S(1)} %collective-permute-done.14.x_ref.refs_12_), channel_id=1, source_target_pairs={{0,2},{1,3},{2,4},{3,5},{4,6},{5,7},{6,8},{7,9},{8,10},{9,11},{10,... | collective-permute-start | bytes 960008 | tf_op jit(solution)/shard_map/ppermute | solution.py:373
  137.1 9.8 %collective-permute-start.15 = (bf16[200,800]{1,0:T(8,128)(2,1)S(1)}, bf16[200,800]{1,0:T(8,128)(2,1)S(1)}, u32[]{:S(2)}, u32[]{:S(2)}) collective-permute-start(bf16[200,800]{1,0:T(8,128)(2,1)S(1)} %collective-permute-done.13.refs_11_), channel_id=1, source_target_pairs={{0,30},{1,31},{2,0},{3,1},{4,2},{5,3},{6,4},{7,5},{8,6},{9,7},{10,... | collective-permute-start | bytes 960008 | tf_op jit(solution)/shard_map/ppermute | solution.py:378
  142.4 8.6 %collective-permute-start.17 = (bf16[200,800]{1,0:T(8,128)(2,1)S(1)}, bf16[200,800]{1,0:T(8,128)(2,1)S(1)}, u32[]{:S(2)}, u32[]{:S(2)}) collective-permute-start(bf16[200,800]{1,0:T(8,128)(2,1)S(1)} %collective-permute-done.16.x_ref.refs_14_), channel_id=1, source_target_pairs={{0,2},{1,3},{2,4},{3,5},{4,6},{5,7},{6,8},{7,9},{8,10},{9,11},{10,... | collective-permute-start | bytes 960008 | tf_op jit(solution)/shard_map/ppermute | solution.py:373
  163.2 1.8 collective-permute-start.18
  172.5 1.8 collective-permute-start.19
  181.8 1.8 collective-permute-start.20
where the time goes:
time: 204 us; the launch traced here: 202 us
  Pallas kernels  70.5 us (35%)
  starting transfers between devices  53.1 us (26%)
  waiting for transfers between devices  41.4 us (20%)
  local copies, waits for them, and re-layouts  18.7 us (9%)
  blocking collectives  16.6 us (8%)
    pallas_call x9, Pallas kernels, exchange_call(): pl.pallas_call(functools.partial(exchange_kernel, occupied, weight, offse...  42.2 us
    pallas_call x3, Pallas kernels, degree_call(): pl.pallas_call(functools.partial(degree_kernel, tuple(offsets), degree, o...  22.7 us
    ppermute x7, starting transfers between devices, body(): left = lax.ppermute(left, 'pts', backward)  21.5 us
    unnamed x28, local copies, waits for them, and re-layouts  17.1 us
    all_to_all x1, starting transfers between devices, body(): lax.all_to_all(sent, 'pts', split_axis=0, concat_axis=0, tiled=True, axis...  17 us
    all_to_all x1, blocking collectives, body(): lax.all_to_all(message, 'pts', split_axis=0, concat_axis=0, tiled=True, a...  16.6 us
    all_to_all x1, waiting for transfers between devices, body(): lax.all_to_all(sent, 'pts', split_axis=0, concat_axis=0, tiled=True, axis...  14.2 us
    all_to_all x1, starting transfers between devices, body(): lax.all_to_all(outgoing, 'pts', split_axis=0, concat_axis=0, tiled=True,...  10 us
  transfers between devices with their start and end apart: 23, of which 15 were waited for; matrix products, arithmetic and copies ran while one was open for 2% of the time, Pallas kernels for 21%

commit v1 on v0

--- a/solution.py
+++ b/solution.py
@@ -342,14 +342,26 @@
     def swap(value):
         return lax.ppermute(value, "pts", swapped)
 
+    def advance(right, left):
+        return lax.ppermute(right, "pts", forward), lax.ppermute(left, "pts", backward)
+
     mate = swap(points_map)
+    rights, lefts = [points_map], [points_map]
+    for value, found in zip(advance(points_map, points_map), (rights, lefts)):
+        found.append(value)
     turned = walkers.reshape(orbitals, walker_count * occupied).T
     trial_blocks = trial.reshape(devices, rows, occupied)
     orbit, near, sent = orbit_call(points_map, mate, turned, trial_blocks)
+    sent, rights[1], lefts[1] = lax.optimization_barrier((sent, rights[1], lefts[1]))
+    for value, found in zip(advance(rights[1], lefts[1]), (rights, lefts)):
+        found.append(value)
     mine = lax.all_to_all(
         sent, "pts", split_axis=0, concat_axis=0, tiled=True, axis_index_groups=same_core
     )
     theirs = swap(mine)
+    mine, rights[2], lefts[2] = lax.optimization_barrier((mine, rights[2], lefts[2]))
+    for value, found in zip(advance(rights[2], lefts[2]), (rights, lefts)):
+        found.append(value)
     cores = split_call(core, rows)
     came = swap(cores[1:2])
     outgoing, hartree = field_call(mine, theirs, cores, draws.T, occupied, columns)
@@ -365,23 +377,21 @@
     partial = jnp.zeros((walker_count, 8, rows), F32)
     partial, fields = lax.optimization_barrier((partial, fields))
     half = chips // 2
-    right = left = points_map
-    blocks, offsets = [points_map], [0]
-    for step in range(half):
-        if step > 1:
+    partial, rights[3], lefts[3] = lax.optimization_barrier((partial, rights[3], lefts[3]))
+    for value, found in zip(advance(rights[3], lefts[3]), (rights, lefts)):
+        found.append(value)
+    for step in range(half + 1):
+        right, left = rights[-1], lefts[-1]
+        if step % 2 and len(rights) <= half:
             right, partial = lax.optimization_barrier((right, partial))
-        after = lax.ppermute(right, "pts", forward)
-        partial = exchange(-step, right, partial, 2.0 if step else 1.0)
-        if step > 1:
+            rights.append(lax.ppermute(right, "pts", forward))
+        weight = 1.0 if step in (0, half) else 2.0
+        partial = exchange(-step, rights[step], partial, weight)
+        if step % 2 and len(lefts) < half:
             left, partial = lax.optimization_barrier((left, partial))
-        if step < half - 1:
-            left = lax.ppermute(left, "pts", backward)
-            blocks.append(left)
-            offsets.append(step + 1)
-        right = after
-        blocks.append(right)
-        offsets.append(-step - 1)
-    partial = exchange(-half, right, partial, 1.0)
+            lefts.append(lax.ppermute(left, "pts", backward))
+    blocks = rights + lefts[1:]
+    offsets = [-step for step in range(half + 1)] + list(range(1, half))
 
     mine, running = degree_call(
         offsets, fields, blocks, 1, occupied, columns, turned, partial, hartree

time: 204 us -> 189 us (0.926)
  blocking collectives: 16.6 us -> 40.2 us
  waiting for transfers between devices: 41.4 us -> 20.9 us
  starting transfers between devices: 53.1 us -> 41.6 us
  local copies, waits for them, and re-layouts: 18.7 us -> 14.1 us
    all_to_all x0 -> x1, blocking collectives: none -> 22 us  [body(): lax.all_to_all(outgoing, 'pts', split_axis=0, concat_axis=0, tiled=True,...]
    all_to_all x1 -> x0, starting transfers between devices: 10 us -> none  [body(): lax.all_to_all(outgoing, 'pts', split_axis=0, concat_axis=0, tiled=True,...]
    all_to_all x1, starting transfers between devices: 17 us -> 7.61 us  [body(): lax.all_to_all(sent, 'pts', split_axis=0, concat_axis=0, tiled=True, axis...]
    all_to_all x1 -> x0, waiting for transfers between devices: 9.36 us -> none  [body(): lax.all_to_all(outgoing, 'pts', split_axis=0, concat_axis=0, tiled=True,...]
    ppermute x15, waiting for transfers between devices: 13.1 us -> 3.81 us  [the longest x4 3.16 us: advance(): lax.ppermute(right, 'pts', forward)]
    ppermute x15, starting transfers between devices: 24.8 us -> 33.2 us  [the longest x4 17.4 us: advance(): lax.ppermute(left, 'pts', backward)]
    unnamed x28 -> x26, local copies, waits for them, and re-layouts: 17.1 us -> 12.5 us
  transfers between devices with their start and end apart: 23 -> 22, of which waited for: 15 -> 7; matrix products, arithmetic and copies ran while one was open for 2% -> 2% of each run, Pallas kernels for 21% -> 25%
where the time goes in v1:
time: 189 us
  Pallas kernels  70.2 us (37%)
  starting transfers between devices  41.6 us (22%)
  blocking collectives  40.2 us (21%)
  waiting for transfers between devices  20.9 us (11%)
  local copies, waits for them, and re-layouts  14.1 us (7%)
    pallas_call x9, Pallas kernels, exchange_call(): pl.pallas_call(functools.partial(exchange_kernel, occupied, weight, offse...  42.4 us
    pallas_call x3, Pallas kernels, degree_call(): pl.pallas_call(functools.partial(degree_kernel, tuple(offsets), degree, o...  22.7 us
    all_to_all x1, blocking collectives, body(): lax.all_to_all(outgoing, 'pts', split_axis=0, concat_axis=0, tiled=True,...  22 us
    all_to_all x1, blocking collectives, body(): lax.all_to_all(message, 'pts', split_axis=0, concat_axis=0, tiled=True, a...  18.2 us
    ppermute x4, starting transfers between devices, advance(): lax.ppermute(left, 'pts', backward)  17.4 us
    unnamed x26, local copies, waits for them, and re-layouts  12.5 us
    all_to_all x1, waiting for transfers between devices, body(): lax.all_to_all(sent, 'pts', split_axis=0, concat_axis=0, tiled=True, axis...  12.4 us
    ppermute x3, starting transfers between devices, body(): lefts.append(lax.ppermute(left, 'pts', backward))  10.2 us
  transfers between devices with their start and end apart: 22, of which 7 were waited for; matrix products, arithmetic and copies ran while one was open for 2% of the time, Pallas kernels for 25%

profile of v1, /device:TPU:70, one launch (start us, length us, event | category | flops | bytes accessed | tf_op | source)
XLA Modules:
  0.0 188.6 jit_solution(8985917954312925924)
XLA Ops:
  0.8 2.2 %collective-permute-start.1 = (bf16[200,800]{1,0:T(8,128)(2,1)}, bf16[200,800]{1,0:T(8,128)(2,1)}, u32[]{:S(2)}, u32[]{:S(2)}) collective-permute-start(bf16[200,800]{1,0:T(8,128)(2,1)} %refs_0_.5), channel_id=1, source_target_pairs={{0,2},{1,3},{2,4},{3,5},{4,6},{5,7},{6,8},{7,9},{8,10},{9,11},{10,... | collective-permute-start | bytes 960008 | tf_op jit(solution)/shard_map/ppermute | solution.py:346
  3.0 10.5 %collective-permute-start.2 = (bf16[200,800]{1,0:T(8,128)(2,1)}, bf16[200,800]{1,0:T(8,128)(2,1)}, u32[]{:S(2)}, u32[]{:S(2)}) collective-permute-start(bf16[200,800]{1,0:T(8,128)(2,1)} %refs_0_.5), channel_id=1, source_target_pairs={{0,30},{1,31},{2,0},{3,1},{4,2},{5,3},{6,4},{7,5},{8,6},{9,7},{10,... | collective-permute-start | bytes 960008 | tf_op jit(solution)/shard_map/ppermute | solution.py:346
  13.5 1.7 copy-done.8
  15.3 1.3 split.1.cores_ref.cores_any
  16.6 1.4 slice.20
  18.0 0.7 copy-done
  18.7 3.3 %copy.8 = bf16[800,12,128]{0,2,1:T(8,128)(2,1)S(1)} copy(bf16[800,12,128]{2,0,1:T(8,128)(2,1)} %param.8) | data formatting | bytes 4915200 | tf_op args[3]
  22.0 0.7 copy-done.9
  22.8 1.4 copy-done.3
  24.2 1.0 copy-done.10
  25.2 2.5 %orbit.1 = (bf16[12,400,128]{2,1,0:T(8,128)(2,1)S(1)}, bf16[400,128]{1,0:T(8,128)(2,1)S(1)}, bf16[16,16,200]{2,1,0:T(8,128)(2,1)}) custom-call(bf16[200,800]{1,0:T(8,128)(2,1)S(1)} %copy-done.7, bf16[200,800]{1,0:T(8,128)(2,1)S(1)} %copy-done.10, bf16[1536,800]{1,0:T(8,128)(2,1)S(1)} %bitcast.7, bf16[32,200,128]{2,1,0:T(8,128)(2,1)S(1)} %bitcast.18), custom_call_target="tpu_custom_call" | custom-call | flops 983040000 | bytes 6000000 | tf_op jit(solution)/shard_map/orbit/pallas_call | solution.py:87
  27.6 1.0 copy-done.5
  28.7 7.6 %all-to-all-start = ((bf16[16,16,200]{2,1,0:T(8,128)(2,1)}), bf16[16,16,200]{2,1,0:T(8,128)(2,1)S(1)}, u32[]{:S(2)}, u32[]{:S(2)}) async-start(bf16[16,16,200]{2,1,0:T(8,128)(2,1)} %get-tuple-element.39), calls=%async_computation | async-start | bytes 262144 | tf_op jit(solution)/shard_map/all_to_all | solution.py:358
  36.3 1.7 collective-permute-start.3
  38.0 1.6 collective-permute-start.4
  39.6 12.4 %all-to-all-done.mine_ref = bf16[16,16,200]{2,1,0:T(8,128)(2,1)S(1)} async-done(((bf16[16,16,200]{2,1,0:T(8,128)(2,1)}), bf16[16,16,200]{2,1,0:T(8,128)(2,1)S(1)}, u32[]{:S(2)}, u32[]{:S(2)}) %all-to-all-start) | async-done | bytes 102432 | tf_op jit(solution)/shard_map/all_to_all | solution.py:358
  52.1 1.5 collective-permute-done.3.x_ref.refs_2_
  53.6 0.4 collective-permute-start.6
  54.0 2.8 %collective-permute-start.7 = (bf16[200,800]{1,0:T(8,128)(2,1)}, bf16[200,800]{1,0:T(8,128)(2,1)S(1)}, u32[]{:S(2)}, u32[]{:S(2)}) collective-permute-start(bf16[200,800]{1,0:T(8,128)(2,1)} %collective-permute-done.4.refs_10_), channel_id=1, source_target_pairs={{0,30},{1,31},{2,0},{3,1},{4,2},{5,3},{6,4},{7,5},{8,6},{9,7},{10,... | collective-permute-start | bytes 960008 | tf_op jit(solution)/shard_map/ppermute | solution.py:346
  56.8 1.9 %copy-done.1 = bf16[2,16,200,200]{3,2,1,0:T(8,128)(2,1)S(1)} copy-done((bf16[2,16,200,200]{3,2,1,0:T(8,128)(2,1)S(1)}, bf16[2,16,200,200]{3,2,1,0:T(8,128)(2,1)}, u32[]{:S(2)}) %copy-start.1) | copy-done | bytes 2560024
  58.8 1.1 field.1
  59.8 22.0 %all_to_all.15.field_ref = f32[16,2,200]{2,1,0:T(2,128)S(1)} all-to-all(f32[16,2,200]{2,1,0:T(2,128)S(1)} %get-tuple-element.43), channel_id=1, replica_groups={{0,2,4,6,8,10,12,14,16,18,20,22,24,26,28,30},{1,3,5,7,9,11,13,15,17,19,..., dimensions={0} | all-to-all | bytes 51200 | tf_op jit(solution)/shard_map/all_to_all | solution.py:368
  81.8 0.8 collective-permute-start.8
  82.6 2.5 %collective-permute-start.11 = (bf16[200,800]{1,0:T(8,128)(2,1)S(1)}, bf16[200,800]{1,0:T(8,128)(2,1)S(1)}, u32[]{:S(2)}, u32[]{:S(2)}) collective-permute-start(bf16[200,800]{1,0:T(8,128)(2,1)S(1)} %collective-permute-done.7.refs_11_), channel_id=1, source_target_pairs={{0,30},{1,31},{2,0},{3,1},{4,2},{5,3},{6,4},{7,5},{8,6},{9,7},{10,... | collective-permute-start | bytes 960008 | tf_op jit(solution)/shard_map/ppermute | solution.py:346
  85.1 4.5 %exchange.9.before_ref = f32[12,8,200]{2,1,0:T(8,128)S(1)} custom-call(bf16[200,800]{1,0:T(8,128)(2,1)S(1)} %copy-done.7, bf16[1536,800]{1,0:T(8,128)(2,1)S(1)} %bitcast.8, bf16[12,400,128]{2,1,0:T(8,128)(2,1)S(1)} %copy-done.6, bf16[400,128]{1,0:T(8,128)(2,1)S(1)} %get-tuple-element.50.near_ref, f32[12,8,200]{2,1,0:T(8,128)S(1)} %broadcast_in_dim.3.before_ref, ...), custom_call_target="tpu_custom_call" | custom-call | flops 983040000 | bytes 5000000 | tf_op jit(solution)/shard_map/exchange/pallas_call | solution.py:208
  89.7 1.6 collective-permute-done.8.x_ref.refs_4_
  91.3 5.5 %exchange.10.before_ref = f32[12,8,200]{2,1,0:T(8,128)S(1)} custom-call(bf16[200,800]{1,0:T(8,128)(2,1)} %collective-permute-done.1.x_ref.refs_1_, bf16[1536,800]{1,0:T(8,128)(2,1)S(1)} %bitcast.9, bf16[12,400,128]{2,1,0:T(8,128)(2,1)S(1)} %copy-done.6, bf16[400,128]{1,0:T(8,128)(2,1)S(1)} %get-tuple-element.50.near_ref, ...), custom_call_target="tpu_custom_call" | custom-call | flops 983040000 | bytes 5000000 | tf_op jit(solution)/shard_map/exchange/pallas_call | solution.py:208
  96.8 3.5 %collective-permute-start.13 = (bf16[200,800]{1,0:T(8,128)(2,1)S(1)}, bf16[200,800]{1,0:T(8,128)(2,1)S(1)}, u32[]{:S(2)}, u32[]{:S(2)}) collective-permute-start(bf16[200,800]{1,0:T(8,128)(2,1)S(1)} %collective-permute-done.11.refs_12_), channel_id=1, source_target_pairs={{0,30},{1,31},{2,0},{3,1},{4,2},{5,3},{6,4},{7,5},{8,6},{9,7},{10,... | collective-permute-start | bytes 960008 | tf_op jit(solution)/shard_map/ppermute | solution.py:392
  100.3 5.5 %exchange.11.before_ref = f32[12,8,200]{2,1,0:T(8,128)S(1)} custom-call(bf16[200,800]{1,0:T(8,128)(2,1)} %collective-permute-done.3.x_ref.refs_2_, bf16[1536,800]{1,0:T(8,128)(2,1)S(1)} %bitcast.10, bf16[12,400,128]{2,1,0:T(8,128)(2,1)S(1)} %copy-done.6, bf16[400,128]{1,0:T(8,128)(2,1)S(1)} %get-tuple-element.50.near_ref, ...), custom_call_target="tpu_custom_call" | custom-call | flops 983040000 | bytes 5000000 | tf_op jit(solution)/shard_map/exchange/pallas_call | solution.py:208
  105.9 4.5 %exchange.12.before_ref = f32[12,8,200]{2,1,0:T(8,128)S(1)} custom-call(bf16[200,800]{1,0:T(8,128)(2,1)S(1)} %collective-permute-done.6.x_ref.refs_3_, bf16[1536,800]{1,0:T(8,128)(2,1)S(1)} %bitcast.11, bf16[12,400,128]{2,1,0:T(8,128)(2,1)S(1)} %copy-done.6, bf16[400,128]{1,0:T(8,128)(2,1)S(1)} %get-tuple-element.50.near_ref, ...), custom_call_target="tpu_custom_call" | custom-call | flops 983040000 | bytes 5000000 | tf_op jit(solution)/shard_map/exchange/pallas_call | solution.py:208
  110.4 3.3 %collective-permute-start.15 = (bf16[200,800]{1,0:T(8,128)(2,1)S(1)}, bf16[200,800]{1,0:T(8,128)(2,1)S(1)}, u32[]{:S(2)}, u32[]{:S(2)}) collective-permute-start(bf16[200,800]{1,0:T(8,128)(2,1)S(1)} %collective-permute-done.13.refs_13_), channel_id=1, source_target_pairs={{0,30},{1,31},{2,0},{3,1},{4,2},{5,3},{6,4},{7,5},{8,6},{9,7},{10,... | collective-permute-start | bytes 960008 | tf_op jit(solution)/shard_map/ppermute | solution.py:392
  113.7 4.5 %exchange.13.before_ref = f32[12,8,200]{2,1,0:T(8,128)S(1)} custom-call(bf16[200,800]{1,0:T(8,128)(2,1)S(1)} %collective-permute-done.8.x_ref.refs_4_, bf16[1536,800]{1,0:T(8,128)(2,1)S(1)} %bitcast.12, bf16[12,400,128]{2,1,0:T(8,128)(2,1)S(1)} %copy-done.6, bf16[400,128]{1,0:T(8,128)(2,1)S(1)} %get-tuple-element.50.near_ref, ...), custom_call_target="tpu_custom_call" | custom-call | flops 983040000 | bytes 5000000 | tf_op jit(solution)/shard_map/exchange/pallas_call | solution.py:208
  118.3 4.5 %exchange.14.before_ref = f32[12,8,200]{2,1,0:T(8,128)S(1)} custom-call(bf16[200,800]{1,0:T(8,128)(2,1)S(1)} %collective-permute-done.10.x_ref.refs_5_, bf16[1536,800]{1,0:T(8,128)(2,1)S(1)} %bitcast.13, bf16[12,400,128]{2,1,0:T(8,128)(2,1)S(1)} %copy-done.6, bf16[400,128]{1,0:T(8,128)(2,1)S(1)} %get-tuple-element.50.near_ref, ...), custom_call_target="tpu_custom_call" | custom-call | flops 983040000 | bytes 5000000 | tf_op jit(solution)/shard_map/exchange/pallas_call | solution.py:208
  122.9 4.5 %exchange.15.before_ref = f32[12,8,200]{2,1,0:T(8,128)S(1)} custom-call(bf16[200,800]{1,0:T(8,128)(2,1)S(1)} %collective-permute-done.12.x_ref.refs_6_, bf16[1536,800]{1,0:T(8,128)(2,1)S(1)} %bitcast.14, bf16[12,400,128]{2,1,0:T(8,128)(2,1)S(1)} %copy-done.6, bf16[400,128]{1,0:T(8,128)(2,1)S(1)} %get-tuple-element.50.near_ref, ...), custom_call_target="tpu_custom_call" | custom-call | flops 983040000 | bytes 5000000 | tf_op jit(solution)/shard_map/exchange/pallas_call | solution.py:208
  127.5 3.5 %collective-permute-start.17 = (bf16[200,800]{1,0:T(8,128)(2,1)S(1)}, bf16[200,800]{1,0:T(8,128)(2,1)S(1)}, u32[]{:S(2)}, u32[]{:S(2)}) collective-permute-start(bf16[200,800]{1,0:T(8,128)(2,1)S(1)} %collective-permute-done.15.refs_14_), channel_id=1, source_target_pairs={{0,30},{1,31},{2,0},{3,1},{4,2},{5,3},{6,4},{7,5},{8,6},{9,7},{10,... | collective-permute-start | bytes 960008 | tf_op jit(solution)/shard_map/ppermute | solution.py:392
  131.0 4.5 %exchange.16.before_ref = f32[12,8,200]{2,1,0:T(8,128)S(1)} custom-call(bf16[200,800]{1,0:T(8,128)(2,1)S(1)} %collective-permute-done.14.x_ref.refs_7_, bf16[1536,800]{1,0:T(8,128)(2,1)S(1)} %bitcast.15, bf16[12,400,128]{2,1,0:T(8,128)(2,1)S(1)} %copy-done.6, bf16[400,128]{1,0:T(8,128)(2,1)S(1)} %get-tuple-element.50.near_ref, ...), custom_call_target="tpu_custom_call" | custom-call | flops 983040000 | bytes 5000000 | tf_op jit(solution)/shard_map/exchange/pallas_call | solution.py:208
  135.5 0.6 collective-permute-done.16.x_ref.refs_8_
  136.1 4.5 %exchange.17.refs_17_ = f32[12,8,200]{2,1,0:T(8,128)S(1)} custom-call(bf16[200,800]{1,0:T(8,128)(2,1)S(1)} %collective-permute-done.16.x_ref.refs_8_, bf16[1536,800]{1,0:T(8,128)(2,1)S(1)} %bitcast.16, bf16[12,400,128]{2,1,0:T(8,128)(2,1)S(1)} %copy-done.6, bf16[400,128]{1,0:T(8,128)(2,1)S(1)} %get-tuple-element.50.near_ref, ...), custom_call_target="tpu_custom_call" | custom-call | flops 983040000 | bytes 5000000 | tf_op jit(solution)/shard_map/exchange/pallas_call | solution.py:208
  140.6 7.7 %degree.3 = (f32[104,800]{1,0:T(8,128)S(1)}, f32[96,800]{1,0:T(8,128)S(1)}) custom-call(f32[16,2,200]{2,1,0:T(2,128)S(1)} %all_to_all.15.field_ref, bf16[200,800]{1,0:T(8,128)(2,1)S(1)} %copy-done.7, bf16[200,800]{1,0:T(8,128)(2,1)} %collective-permute-done.1.x_ref.refs_1_, bf16[200,800]{1,0:T(8,128)(2,1)} %collective-permute-done.3.x_ref.refs_2_, ...), custom_call_target="tpu_custom_call" | custom-call | flops 983040000 | bytes 6000000 | tf_op jit(solution)/shard_map/degree/pallas_call | solution.py:279
  148.5 1.7 collective-permute-done.18.refs_17_
  150.1 7.5 %degree.4 = (f32[96,800]{1,0:T(8,128)S(1)}, f32[96,800]{1,0:T(8,128)S(1)}) custom-call(f32[16,2,200]{2,1,0:T(2,128)S(1)} %all_to_all.15.field_ref, bf16[200,800]{1,0:T(8,128)(2,1)S(1)} %copy-done.7, bf16[200,800]{1,0:T(8,128)(2,1)} %collective-permute-done.1.x_ref.refs_1_, bf16[200,800]{1,0:T(8,128)(2,1)} %collective-permute-done.3.x_ref.refs_2_, ...), custom_call_target="tpu_custom_call" | custom-call | flops 983040000 | bytes 6000000 | tf_op jit(solution)/shard_map/degree/pallas_call | solution.py:279
  157.7 0.3 collective-permute-start.19
  157.9 1.5 collective-permute-done.19.refs_17_
  159.4 7.5 %degree.5 = (f32[96,800]{1,0:T(8,128)S(1)}, f32[96,800]{1,0:T(8,128)S(1)}) custom-call(f32[16,2,200]{2,1,0:T(2,128)S(1)} %all_to_all.15.field_ref, bf16[200,800]{1,0:T(8,128)(2,1)S(1)} %copy-done.7, bf16[200,800]{1,0:T(8,128)(2,1)} %collective-permute-done.1.x_ref.refs_1_, bf16[200,800]{1,0:T(8,128)(2,1)} %collective-permute-done.3.x_ref.refs_2_, ...), custom_call_target="tpu_custom_call" | custom-call | flops 983040000 | bytes 6000000 | tf_op jit(solution)/shard_map/degree/pallas_call | solution.py:279
  167.2 1.5 collective-permute-done.20.other_ref
  168.9 18.2 %all_to_all.16 = bf16[16,25,128]{2,1,0:T(8,128)(2,1)S(1)} all-to-all(bf16[16,25,128]{2,1,0:T(8,128)(2,1)S(1)} %finish.1), channel_id=1, replica_groups={{0,2,4,6,8,10,12,14,16,18,20,22,24,26,28,30},{1,3,5,7,9,11,13,15,17,19,..., dimensions={0} | all-to-all | bytes 204800 | tf_op jit(solution)/shard_map/all_to_all | solution.py:407
  187.3 0.7 copy.10
  188.0 0.6 convert_reduce_fusion
  (48 shorter events, 1.4 us)
Async XLA Ops:
  0.6 21.4 %collective-permute-start = (bf16[200,800]{1,0:T(8,128)(2,1)}, bf16[200,800]{1,0:T(8,128)(2,1)S(1)}, u32[]{:S(2)}, u32[]{:S(2)}) collective-permute-start(bf16[200,800]{1,0:T(8,128)(2,1)} %refs_0_.5), channel_id=1, source_target_pairs={{0,1},{1,0},{2,3},{3,2},{4,5},{5,4},{6,7},{7,6},{8,9},{9,8},{10,11... | collective-permute-start | bytes 960008 | tf_op jit(solution)/shard_map/ppermute | solution.py:343
  0.8 27.9 %collective-permute-start.1 = (bf16[200,800]{1,0:T(8,128)(2,1)}, bf16[200,800]{1,0:T(8,128)(2,1)}, u32[]{:S(2)}, u32[]{:S(2)}) collective-permute-start(bf16[200,800]{1,0:T(8,128)(2,1)} %refs_0_.5), channel_id=1, source_target_pairs={{0,2},{1,3},{2,4},{3,5},{4,6},{5,7},{6,8},{7,9},{8,10},{9,11},{10,... | collective-permute-start | bytes 960008 | tf_op jit(solution)/shard_map/ppermute | solution.py:346
  3.0 25.7 %collective-permute-start.2 = (bf16[200,800]{1,0:T(8,128)(2,1)}, bf16[200,800]{1,0:T(8,128)(2,1)}, u32[]{:S(2)}, u32[]{:S(2)}) collective-permute-start(bf16[200,800]{1,0:T(8,128)(2,1)} %refs_0_.5), channel_id=1, source_target_pairs={{0,30},{1,31},{2,0},{3,1},{4,2},{5,3},{6,4},{7,5},{8,6},{9,7},{10,... | collective-permute-start | bytes 960008 | tf_op jit(solution)/shard_map/ppermute | solution.py:346
  13.5 1.7 copy-start.8
  16.5 2.2 %copy-start = (bf16[2,16,200,200]{3,2,1,0:T(8,128)(2,1)}, bf16[2,16,200,200]{3,2,1,0:T(8,128)(2,1)S(1)}, u32[]{:S(2)}) copy-start(bf16[2,16,200,200]{3,2,1,0:T(8,128)(2,1)S(1)} %split.1.cores_ref.cores_any) | copy-start | bytes 7680004
  18.7 4.0 %copy-start.7 = (bf16[200,800]{1,0:T(8,128)(2,1)S(1)}, bf16[200,800]{1,0:T(8,128)(2,1)}, u32[]{:S(2)}) copy-start(bf16[200,800]{1,0:T(8,128)(2,1)} %refs_0_.5) | copy-start | bytes 960004
  18.7 66.4 %collective-permute-start.9 = (bf16[1,16,200,200]{3,2,1,0:T(8,128)(2,1)}, bf16[1,16,200,200]{3,2,1,0:T(8,128)(2,1)}, u32[]{:S(2)}, u32[]{:S(2)}) collective-permute-start(bf16[1,16,200,200]{3,2,1,0:T(8,128)(2,1)} %slice.20), channel_id=1, source_target_pairs={{0,1},{1,0},{2,3},{3,2},{4,5},{5,4},{6,7},{7,6},{8,9},{9,8},{10,11... | collective-permute-start | bytes 3840008 | tf_op jit(solution)/shard_map/ppermute | solution.py:343
  22.0 0.7 copy-start.9
  22.7 1.4 copy-start.3
  24.2 1.0 copy-start.10
  25.2 31.7 %copy-start.11 = (s32[200,12]{0,1:T(8,128)S(1)}, s32[200,12]{0,1:T(8,128)}, u32[]{:S(2)}) copy-start(s32[200,12]{0,1:T(8,128)} %param.9) | copy-start | bytes 28804
  27.6 1.0 copy-start.5
  28.7 23.4 %all-to-all-start = ((bf16[16,16,200]{2,1,0:T(8,128)(2,1)}), bf16[16,16,200]{2,1,0:T(8,128)(2,1)S(1)}, u32[]{:S(2)}, u32[]{:S(2)}) async-start(bf16[16,16,200]{2,1,0:T(8,128)(2,1)} %get-tuple-element.39), calls=%async_computation | async-start | bytes 262144 | tf_op jit(solution)/shard_map/all_to_all | solution.py:358
  36.3 17.3 %collective-permute-start.3 = (bf16[200,800]{1,0:T(8,128)(2,1)}, bf16[200,800]{1,0:T(8,128)(2,1)}, u32[]{:S(2)}, u32[]{:S(2)}) collective-permute-start(bf16[200,800]{1,0:T(8,128)(2,1)} %collective-permute-done.1.x_ref.refs_1_), channel_id=1, source_target_pairs={{0,2},{1,3},{2,4},{3,5},{4,6},{5,7},{6,8},{7,9},{8,10},{9,11},{10,... | collective-permute-start | bytes 960008 | tf_op jit(solution)/shard_map/ppermute | solution.py:346
  38.0 15.6 %collective-permute-start.4 = (bf16[200,800]{1,0:T(8,128)(2,1)}, bf16[200,800]{1,0:T(8,128)(2,1)}, u32[]{:S(2)}, u32[]{:S(2)}) collective-permute-start(bf16[200,800]{1,0:T(8,128)(2,1)} %collective-permute-done.2.refs_9_), channel_id=1, source_target_pairs={{0,30},{1,31},{2,0},{3,1},{4,2},{5,3},{6,4},{7,5},{8,6},{9,7},{10,... | collective-permute-start | bytes 960008 | tf_op jit(solution)/shard_map/ppermute | solution.py:346
  52.1 4.8 %collective-permute-start.5 = (bf16[16,16,200]{2,1,0:T(8,128)(2,1)S(1)}, bf16[16,16,200]{2,1,0:T(8,128)(2,1)S(1)}, u32[]{:S(2)}, u32[]{:S(2)}) collective-permute-start(bf16[16,16,200]{2,1,0:T(8,128)(2,1)S(1)} %all-to-all-done.mine_ref), channel_id=1, source_target_pairs={{0,1},{1,0},{2,3},{3,2},{4,5},{5,4},{6,7},{7,6},{8,9},{9,8},{10,11... | collective-permute-start | bytes 307208 | tf_op jit(solution)/shard_map/ppermute | solution.py:343
  53.6 28.2 %collective-permute-start.6 = (bf16[200,800]{1,0:T(8,128)(2,1)}, bf16[200,800]{1,0:T(8,128)(2,1)S(1)}, u32[]{:S(2)}, u32[]{:S(2)}) collective-permute-start(bf16[200,800]{1,0:T(8,128)(2,1)} %collective-permute-done.3.x_ref.refs_2_), channel_id=1, source_target_pairs={{0,2},{1,3},{2,4},{3,5},{4,6},{5,7},{6,8},{7,9},{8,10},{9,11},{10,... | collective-permute-start | bytes 960008 | tf_op jit(solution)/shard_map/ppermute | solution.py:346
  54.0 27.8 %collective-permute-start.7 = (bf16[200,800]{1,0:T(8,128)(2,1)}, bf16[200,800]{1,0:T(8,128)(2,1)S(1)}, u32[]{:S(2)}, u32[]{:S(2)}) collective-permute-start(bf16[200,800]{1,0:T(8,128)(2,1)} %collective-permute-done.4.refs_10_), channel_id=1, source_target_pairs={{0,30},{1,31},{2,0},{3,1},{4,2},{5,3},{6,4},{7,5},{8,6},{9,7},{10,... | collective-permute-start | bytes 960008 | tf_op jit(solution)/shard_map/ppermute | solution.py:346
  56.8 1.9 %copy-start.1 = (bf16[2,16,200,200]{3,2,1,0:T(8,128)(2,1)S(1)}, bf16[2,16,200,200]{3,2,1,0:T(8,128)(2,1)}, u32[]{:S(2)}) copy-start(bf16[2,16,200,200]{3,2,1,0:T(8,128)(2,1)} %copy-done) | copy-start | bytes 7680004
  58.8 26.3 %copy-start.2 = (bf16[2,16,200,200]{3,2,1,0:T(8,128)(2,1)S(1)}, bf16[2,16,200,200]{3,2,1,0:T(8,128)(2,1)}, u32[]{:S(2)}) copy-start(bf16[2,16,200,200]{3,2,1,0:T(8,128)(2,1)} %copy-done) | copy-start | bytes 7680004
  58.8 26.3 %copy-start.4 = (bf16[6400,128]{1,0:T(8,128)(2,1)S(1)}, bf16[6400,128]{1,0:T(8,128)(2,1)}, u32[]{:S(2)}) copy-start(bf16[6400,128]{1,0:T(8,128)(2,1)} %param.6) | copy-start | bytes 4915204
  58.8 26.3 %copy-start.6 = (bf16[12,400,128]{2,1,0:T(8,128)(2,1)S(1)}, bf16[12,400,128]{2,1,0:T(8,128)(2,1)}, u32[]{:S(2)}) copy-start(bf16[12,400,128]{2,1,0:T(8,128)(2,1)} %copy-done.5) | copy-start | bytes 3686404
  81.8 9.4 %collective-permute-start.8 = (bf16[200,800]{1,0:T(8,128)(2,1)S(1)}, bf16[200,800]{1,0:T(8,128)(2,1)S(1)}, u32[]{:S(2)}, u32[]{:S(2)}) collective-permute-start(bf16[200,800]{1,0:T(8,128)(2,1)S(1)} %collective-permute-done.6.x_ref.refs_3_), channel_id=1, source_target_pairs={{0,2},{1,3},{2,4},{3,5},{4,6},{5,7},{6,8},{7,9},{8,10},{9,11},{10,... | collective-permute-start | bytes 960008 | tf_op jit(solution)/shard_map/ppermute | solution.py:346
  82.6 14.1 %collective-permute-start.11 = (bf16[200,800]{1,0:T(8,128)(2,1)S(1)}, bf16[200,800]{1,0:T(8,128)(2,1)S(1)}, u32[]{:S(2)}, u32[]{:S(2)}) collective-permute-start(bf16[200,800]{1,0:T(8,128)(2,1)S(1)} %collective-permute-done.7.refs_11_), channel_id=1, source_target_pairs={{0,30},{1,31},{2,0},{3,1},{4,2},{5,3},{6,4},{7,5},{8,6},{9,7},{10,... | collective-permute-start | bytes 960008 | tf_op jit(solution)/shard_map/ppermute | solution.py:346
  91.3 14.5 %collective-permute-start.10 = (bf16[200,800]{1,0:T(8,128)(2,1)S(1)}, bf16[200,800]{1,0:T(8,128)(2,1)S(1)}, u32[]{:S(2)}, u32[]{:S(2)}) collective-permute-start(bf16[200,800]{1,0:T(8,128)(2,1)S(1)} %collective-permute-done.8.x_ref.refs_4_), channel_id=1, source_target_pairs={{0,2},{1,3},{2,4},{3,5},{4,6},{5,7},{6,8},{7,9},{8,10},{9,11},{10,... | collective-permute-start | bytes 960008 | tf_op jit(solution)/shard_map/ppermute | solution.py:387
  96.8 13.7 %collective-permute-start.13 = (bf16[200,800]{1,0:T(8,128)(2,1)S(1)}, bf16[200,800]{1,0:T(8,128)(2,1)S(1)}, u32[]{:S(2)}, u32[]{:S(2)}) collective-permute-start(bf16[200,800]{1,0:T(8,128)(2,1)S(1)} %collective-permute-done.11.refs_12_), channel_id=1, source_target_pairs={{0,30},{1,31},{2,0},{3,1},{4,2},{5,3},{6,4},{7,5},{8,6},{9,7},{10,... | collective-permute-start | bytes 960008 | tf_op jit(solution)/shard_map/ppermute | solution.py:392
  105.8 12.4 %collective-permute-start.12 = (bf16[200,800]{1,0:T(8,128)(2,1)S(1)}, bf16[200,800]{1,0:T(8,128)(2,1)S(1)}, u32[]{:S(2)}, u32[]{:S(2)}) collective-permute-start(bf16[200,800]{1,0:T(8,128)(2,1)S(1)} %collective-permute-done.10.x_ref.refs_5_), channel_id=1, source_target_pairs={{0,2},{1,3},{2,4},{3,5},{4,6},{5,7},{6,8},{7,9},{8,10},{9,11},{10,... | collective-permute-start | bytes 960008 | tf_op jit(solution)/shard_map/ppermute | solution.py:387
  110.4 12.4 %collective-permute-start.15 = (bf16[200,800]{1,0:T(8,128)(2,1)S(1)}, bf16[200,800]{1,0:T(8,128)(2,1)S(1)}, u32[]{:S(2)}, u32[]{:S(2)}) collective-permute-start(bf16[200,800]{1,0:T(8,128)(2,1)S(1)} %collective-permute-done.13.refs_13_), channel_id=1, source_target_pairs={{0,30},{1,31},{2,0},{3,1},{4,2},{5,3},{6,4},{7,5},{8,6},{9,7},{10,... | collective-permute-start | bytes 960008 | tf_op jit(solution)/shard_map/ppermute | solution.py:392
  118.2 9.2 %collective-permute-start.14 = (bf16[200,800]{1,0:T(8,128)(2,1)S(1)}, bf16[200,800]{1,0:T(8,128)(2,1)S(1)}, u32[]{:S(2)}, u32[]{:S(2)}) collective-permute-start(bf16[200,800]{1,0:T(8,128)(2,1)S(1)} %collective-permute-done.12.x_ref.refs_6_), channel_id=1, source_target_pairs={{0,2},{1,3},{2,4},{3,5},{4,6},{5,7},{6,8},{7,9},{8,10},{9,11},{10,... | collective-permute-start | bytes 960008 | tf_op jit(solution)/shard_map/ppermute | solution.py:387
  127.4 8.7 %collective-permute-start.16 = (bf16[200,800]{1,0:T(8,128)(2,1)S(1)}, bf16[200,800]{1,0:T(8,128)(2,1)S(1)}, u32[]{:S(2)}, u32[]{:S(2)}) collective-permute-start(bf16[200,800]{1,0:T(8,128)(2,1)S(1)} %collective-permute-done.14.x_ref.refs_7_), channel_id=1, source_target_pairs={{0,2},{1,3},{2,4},{3,5},{4,6},{5,7},{6,8},{7,9},{8,10},{9,11},{10,... | collective-permute-start | bytes 960008 | tf_op jit(solution)/shard_map/ppermute | solution.py:387
  127.5 13.1 %collective-permute-start.17 = (bf16[200,800]{1,0:T(8,128)(2,1)S(1)}, bf16[200,800]{1,0:T(8,128)(2,1)S(1)}, u32[]{:S(2)}, u32[]{:S(2)}) collective-permute-start(bf16[200,800]{1,0:T(8,128)(2,1)S(1)} %collective-permute-done.15.refs_14_), channel_id=1, source_target_pairs={{0,30},{1,31},{2,0},{3,1},{4,2},{5,3},{6,4},{7,5},{8,6},{9,7},{10,... | collective-permute-start | bytes 960008 | tf_op jit(solution)/shard_map/ppermute | solution.py:392
  148.3 1.8 collective-permute-start.18
  157.7 1.8 collective-permute-start.19
  166.9 1.8 collective-permute-start.20

commit v2 on v1

--- a/solution.py
+++ b/solution.py
@@ -349,21 +349,23 @@
     rights, lefts = [points_map], [points_map]
     for value, found in zip(advance(points_map, points_map), (rights, lefts)):
         found.append(value)
+    cores = split_call(core, rows)
+    came = swap(cores[1:2])
+    walkers, cores, rights[1], lefts[1] = lax.optimization_barrier(
+        (walkers, cores, rights[1], lefts[1])
+    )
+    for value, found in zip(advance(rights[1], lefts[1]), (rights, lefts)):
+        found.append(value)
     turned = walkers.reshape(orbitals, walker_count * occupied).T
     trial_blocks = trial.reshape(devices, rows, occupied)
     orbit, near, sent = orbit_call(points_map, mate, turned, trial_blocks)
-    sent, rights[1], lefts[1] = lax.optimization_barrier((sent, rights[1], lefts[1]))
-    for value, found in zip(advance(rights[1], lefts[1]), (rights, lefts)):
-        found.append(value)
+    sent, rights[2], lefts[2] = lax.optimization_barrier((sent, rights[2], lefts[2]))
     mine = lax.all_to_all(
         sent, "pts", split_axis=0, concat_axis=0, tiled=True, axis_index_groups=same_core
     )
     theirs = swap(mine)
-    mine, rights[2], lefts[2] = lax.optimization_barrier((mine, rights[2], lefts[2]))
     for value, found in zip(advance(rights[2], lefts[2]), (rights, lefts)):
         found.append(value)
-    cores = split_call(core, rows)
-    came = swap(cores[1:2])
     outgoing, hartree = field_call(mine, theirs, cores, draws.T, occupied, columns)
     fields = lax.all_to_all(
         outgoing, "pts", split_axis=0, concat_axis=0, tiled=True, axis_index_groups=same_core

time: 189 us -> 184 us (0.974)
  blocking collectives: 40.2 us -> 56.8 us
  starting transfers between devices: 41.6 us -> 33.8 us
  waiting for transfers between devices: 20.9 us -> 13.2 us
  local copies, waits for them, and re-layouts: 14.1 us -> 8.56 us
    all_to_all x0 -> x1, blocking collectives: none -> 21.5 us  [body(): lax.all_to_all(sent, 'pts', split_axis=0, concat_axis=0, tiled=True, axis...]
    all_to_all x1 -> x0, waiting for transfers between devices: 12.4 us -> none  [body(): lax.all_to_all(sent, 'pts', split_axis=0, concat_axis=0, tiled=True, axis...]
    unnamed x26 -> x13, local copies, waits for them, and re-layouts: 12.5 us -> 3.83 us
    all_to_all x1 -> x0, starting transfers between devices: 7.61 us -> none  [body(): lax.all_to_all(sent, 'pts', split_axis=0, concat_axis=0, tiled=True, axis...]
    all_to_all x1, blocking collectives: 22 us -> 17.1 us  [body(): lax.all_to_all(outgoing, 'pts', split_axis=0, concat_axis=0, tiled=True,...]
    ppermute x4, waiting for transfers between devices: 3.16 us -> 7.85 us  [advance(): lax.ppermute(right, 'pts', forward)]
    optimization_barrier x0 -> x1, local copies, waits for them, and re-layouts: none -> 3.27 us  [body(): lax.optimization_barrier((walkers, cores, rights[1], lefts[1]))]
  transfers between devices with their start and end apart: 22 -> 21, of which waited for: 7 -> 6; matrix products, arithmetic and copies ran while one was open for 2% -> 2% of each run, Pallas kernels for 25% -> 26%
where the time goes in v2:
time: 184 us; the launch traced here: 183 us
  Pallas kernels  69.4 us (38%)
  blocking collectives  56.8 us (31%)
  starting transfers between devices  33.8 us (18%)
  waiting for transfers between devices  13.2 us (7%)
  local copies, waits for them, and re-layouts  8.56 us (5%)
    pallas_call x9, Pallas kernels, exchange_call(): pl.pallas_call(functools.partial(exchange_kernel, occupied, weight, offse...  41.5 us
    pallas_call x3, Pallas kernels, degree_call(): pl.pallas_call(functools.partial(degree_kernel, tuple(offsets), degree, o...  22.4 us
    all_to_all x1, blocking collectives, body(): lax.all_to_all(sent, 'pts', split_axis=0, concat_axis=0, tiled=True, axis...  21.5 us
    all_to_all x1, blocking collectives, body(): lax.all_to_all(message, 'pts', split_axis=0, concat_axis=0, tiled=True, a...  18.2 us
    ppermute x4, starting transfers between devices, advance(): lax.ppermute(left, 'pts', backward)  17.6 us
    all_to_all x1, blocking collectives, body(): lax.all_to_all(outgoing, 'pts', split_axis=0, concat_axis=0, tiled=True,...  17.1 us
    ppermute x3, starting transfers between devices, body(): lefts.append(lax.ppermute(left, 'pts', backward))  10.2 us
    ppermute x4, waiting for transfers between devices, advance(): lax.ppermute(right, 'pts', forward)  7.85 us
  transfers between devices with their start and end apart: 21, of which 6 were waited for; matrix products, arithmetic and copies ran while one was open for 2% of the time, Pallas kernels for 26%

profile of v2, /device:TPU:70, one launch (start us, length us, event | category | flops | bytes accessed | tf_op | source)
XLA Modules:
  0.0 183.2 jit_solution(1631593627773973048)
XLA Ops:
  0.6 2.2 %collective-permute-start.1 = (bf16[200,800]{1,0:T(8,128)(2,1)}, bf16[200,800]{1,0:T(8,128)(2,1)S(1)}, u32[]{:S(2)}, u32[]{:S(2)}) collective-permute-start(bf16[200,800]{1,0:T(8,128)(2,1)} %refs_0_.5), channel_id=1, source_target_pairs={{0,2},{1,3},{2,4},{3,5},{4,6},{5,7},{6,8},{7,9},{8,10},{9,11},{10,... | collective-permute-start | bytes 960008 | tf_op jit(solution)/shard_map/ppermute | solution.py:346
  2.9 10.5 %collective-permute-start.2 = (bf16[200,800]{1,0:T(8,128)(2,1)}, bf16[200,800]{1,0:T(8,128)(2,1)}, u32[]{:S(2)}, u32[]{:S(2)}) collective-permute-start(bf16[200,800]{1,0:T(8,128)(2,1)} %refs_0_.5), channel_id=1, source_target_pairs={{0,30},{1,31},{2,0},{3,1},{4,2},{5,3},{6,4},{7,5},{8,6},{9,7},{10,... | collective-permute-start | bytes 960008 | tf_op jit(solution)/shard_map/ppermute | solution.py:346
  13.4 1.7 copy-done.4
  15.1 1.3 split.1.cores_ref.cores_any
  16.4 5.5 %collective-permute-done.1.x_ref.refs_1_ = bf16[200,800]{1,0:T(8,128)(2,1)S(1)} collective-permute-done((bf16[200,800]{1,0:T(8,128)(2,1)}, bf16[200,800]{1,0:T(8,128)(2,1)S(1)}, u32[]{:S(2)}, u32[]{:S(2)}) %collective-permute-start.1) | collective-permute-done | bytes 320032 | tf_op jit(solution)/shard_map/ppermute | solution.py:346
  21.9 3.2 %collective-permute-start.4 = (bf16[200,800]{1,0:T(8,128)(2,1)}, bf16[200,800]{1,0:T(8,128)(2,1)}, u32[]{:S(2)}, u32[]{:S(2)}) collective-permute-start(bf16[200,800]{1,0:T(8,128)(2,1)} %collective-permute-done.2.refs_9_), channel_id=1, source_target_pairs={{0,30},{1,31},{2,0},{3,1},{4,2},{5,3},{6,4},{7,5},{8,6},{9,7},{10,... | collective-permute-start | bytes 960008 | tf_op jit(solution)/shard_map/ppermute | solution.py:346
  25.2 1.3 slice.20
  26.4 3.3 %copy.8 = bf16[800,12,128]{0,2,1:T(8,128)(2,1)S(1)} copy(bf16[800,12,128]{2,0,1:T(8,128)(2,1)} %param.8) | data formatting | bytes 4915200 | tf_op jit(solution)/shard_map/optimization_barrier | solution.py:354
  29.7 1.4 copy-done.2
  31.2 2.9 %orbit.1 = (bf16[12,400,128]{2,1,0:T(8,128)(2,1)S(1)}, bf16[400,128]{1,0:T(8,128)(2,1)S(1)}, bf16[16,16,200]{2,1,0:T(8,128)(2,1)S(1)}) custom-call(bf16[200,800]{1,0:T(8,128)(2,1)S(1)} %copy-done.3, bf16[200,800]{1,0:T(8,128)(2,1)} %collective-permute-done.mate_ref, bf16[1536,800]{1,0:T(8,128)(2,1)S(1)} %bitcast.7, bf16[32,200,128]{2,1,0:T(8,128)(2,1)S(1)} %bitcast.18), custom_call_target="tpu_custom_call" | custom-call | flops 983040000 | bytes 6000000 | tf_op jit(solution)/shard_map/orbit/pallas_call | solution.py:87
  34.1 21.5 %all_to_all.15.mine_ref = bf16[16,16,200]{2,1,0:T(8,128)(2,1)S(1)} all-to-all(bf16[16,16,200]{2,1,0:T(8,128)(2,1)S(1)} %get-tuple-element.43), channel_id=1, replica_groups={{0,2,4,6,8,10,12,14,16,18,20,22,24,26,28,30},{1,3,5,7,9,11,13,15,17,19,..., dimensions={0} | all-to-all | bytes 204800 | tf_op jit(solution)/shard_map/all_to_all | solution.py:363
  55.6 2.0 %collective-permute-start.6 = (bf16[200,800]{1,0:T(8,128)(2,1)}, bf16[200,800]{1,0:T(8,128)(2,1)S(1)}, u32[]{:S(2)}, u32[]{:S(2)}) collective-permute-start(bf16[200,800]{1,0:T(8,128)(2,1)} %collective-permute-done.3.x_ref.refs_2_), channel_id=1, source_target_pairs={{0,2},{1,3},{2,4},{3,5},{4,6},{5,7},{6,8},{7,9},{8,10},{9,11},{10,... | collective-permute-start | bytes 960008 | tf_op jit(solution)/shard_map/ppermute | solution.py:346
  57.5 1.3 collective-permute-start.7
  58.8 1.1 field.1
  59.9 17.1 %all_to_all.16.field_ref = f32[16,2,200]{2,1,0:T(2,128)S(1)} all-to-all(f32[16,2,200]{2,1,0:T(2,128)S(1)} %get-tuple-element.45), channel_id=1, replica_groups={{0,2,4,6,8,10,12,14,16,18,20,22,24,26,28,30},{1,3,5,7,9,11,13,15,17,19,..., dimensions={0} | all-to-all | bytes 51200 | tf_op jit(solution)/shard_map/all_to_all | solution.py:370
  77.0 0.7 collective-permute-start.8
  77.8 2.5 %collective-permute-start.11 = (bf16[200,800]{1,0:T(8,128)(2,1)S(1)}, bf16[200,800]{1,0:T(8,128)(2,1)S(1)}, u32[]{:S(2)}, u32[]{:S(2)}) collective-permute-start(bf16[200,800]{1,0:T(8,128)(2,1)S(1)} %collective-permute-done.7.refs_11_), channel_id=1, source_target_pairs={{0,30},{1,31},{2,0},{3,1},{4,2},{5,3},{6,4},{7,5},{8,6},{9,7},{10,... | collective-permute-start | bytes 960008 | tf_op jit(solution)/shard_map/ppermute | solution.py:346
  80.3 4.5 %exchange.9.before_ref = f32[12,8,200]{2,1,0:T(8,128)S(1)} custom-call(bf16[200,800]{1,0:T(8,128)(2,1)S(1)} %copy-done.3, bf16[1536,800]{1,0:T(8,128)(2,1)S(1)} %bitcast.8, bf16[12,400,128]{2,1,0:T(8,128)(2,1)S(1)} %get-tuple-element.51.orbit_ref, bf16[400,128]{1,0:T(8,128)(2,1)S(1)} %get-tuple-element.52.near_ref, ...), custom_call_target="tpu_custom_call" | custom-call | flops 983040000 | bytes 5000000 | tf_op jit(solution)/shard_map/exchange/pallas_call | solution.py:208
  84.8 2.3 %collective-permute-done.8.x_ref.refs_4_ = bf16[200,800]{1,0:T(8,128)(2,1)S(1)} collective-permute-done((bf16[200,800]{1,0:T(8,128)(2,1)S(1)}, bf16[200,800]{1,0:T(8,128)(2,1)S(1)}, u32[]{:S(2)}, u32[]{:S(2)}) %collective-permute-start.8) | collective-permute-done | bytes 320032 | tf_op jit(solution)/shard_map/ppermute | solution.py:346
  87.1 4.5 %exchange.10.before_ref = f32[12,8,200]{2,1,0:T(8,128)S(1)} custom-call(bf16[200,800]{1,0:T(8,128)(2,1)S(1)} %collective-permute-done.1.x_ref.refs_1_, bf16[1536,800]{1,0:T(8,128)(2,1)S(1)} %bitcast.9, bf16[12,400,128]{2,1,0:T(8,128)(2,1)S(1)} %get-tuple-element.51.orbit_ref, bf16[400,128]{1,0:T(8,128)(2,1)S(1)} %get-tuple-element.52.near_ref, ...), custom_call_target="tpu_custom_call" | custom-call | flops 983040000 | bytes 5000000 | tf_op jit(solution)/shard_map/exchange/pallas_call | solution.py:208
  91.7 3.5 %collective-permute-start.13 = (bf16[200,800]{1,0:T(8,128)(2,1)S(1)}, bf16[200,800]{1,0:T(8,128)(2,1)S(1)}, u32[]{:S(2)}, u32[]{:S(2)}) collective-permute-start(bf16[200,800]{1,0:T(8,128)(2,1)S(1)} %collective-permute-done.11.refs_12_), channel_id=1, source_target_pairs={{0,30},{1,31},{2,0},{3,1},{4,2},{5,3},{6,4},{7,5},{8,6},{9,7},{10,... | collective-permute-start | bytes 960008 | tf_op jit(solution)/shard_map/ppermute | solution.py:394
  95.2 5.5 %exchange.11.before_ref = f32[12,8,200]{2,1,0:T(8,128)S(1)} custom-call(bf16[200,800]{1,0:T(8,128)(2,1)} %collective-permute-done.3.x_ref.refs_2_, bf16[1536,800]{1,0:T(8,128)(2,1)S(1)} %bitcast.10, bf16[12,400,128]{2,1,0:T(8,128)(2,1)S(1)} %get-tuple-element.51.orbit_ref, bf16[400,128]{1,0:T(8,128)(2,1)S(1)} %get-tuple-element.52.near_ref, ...), custom_call_target="tpu_custom_call" | custom-call | flops 983040000 | bytes 5000000 | tf_op jit(solution)/shard_map/exchange/pallas_call | solution.py:208
  100.6 0.1 collective-permute-start.12
  100.8 4.5 %exchange.12.before_ref = f32[12,8,200]{2,1,0:T(8,128)S(1)} custom-call(bf16[200,800]{1,0:T(8,128)(2,1)S(1)} %collective-permute-done.6.x_ref.refs_3_, bf16[1536,800]{1,0:T(8,128)(2,1)S(1)} %bitcast.11, bf16[12,400,128]{2,1,0:T(8,128)(2,1)S(1)} %get-tuple-element.51.orbit_ref, bf16[400,128]{1,0:T(8,128)(2,1)S(1)} %get-tuple-element.52.near_ref, ...), custom_call_target="tpu_custom_call" | custom-call | flops 983040000 | bytes 5000000 | tf_op jit(solution)/shard_map/exchange/pallas_call | solution.py:208
  105.3 3.3 %collective-permute-start.15 = (bf16[200,800]{1,0:T(8,128)(2,1)S(1)}, bf16[200,800]{1,0:T(8,128)(2,1)S(1)}, u32[]{:S(2)}, u32[]{:S(2)}) collective-permute-start(bf16[200,800]{1,0:T(8,128)(2,1)S(1)} %collective-permute-done.13.refs_13_), channel_id=1, source_target_pairs={{0,30},{1,31},{2,0},{3,1},{4,2},{5,3},{6,4},{7,5},{8,6},{9,7},{10,... | collective-permute-start | bytes 960008 | tf_op jit(solution)/shard_map/ppermute | solution.py:394
  108.6 4.5 %exchange.13.before_ref = f32[12,8,200]{2,1,0:T(8,128)S(1)} custom-call(bf16[200,800]{1,0:T(8,128)(2,1)S(1)} %collective-permute-done.8.x_ref.refs_4_, bf16[1536,800]{1,0:T(8,128)(2,1)S(1)} %bitcast.12, bf16[12,400,128]{2,1,0:T(8,128)(2,1)S(1)} %get-tuple-element.51.orbit_ref, bf16[400,128]{1,0:T(8,128)(2,1)S(1)} %get-tuple-element.52.near_ref, ...), custom_call_target="tpu_custom_call" | custom-call | flops 983040000 | bytes 5000000 | tf_op jit(solution)/shard_map/exchange/pallas_call | solution.py:208
  113.1 0.1 collective-permute-start.14
  113.2 4.5 %exchange.14.before_ref = f32[12,8,200]{2,1,0:T(8,128)S(1)} custom-call(bf16[200,800]{1,0:T(8,128)(2,1)S(1)} %collective-permute-done.10.x_ref.refs_5_, bf16[1536,800]{1,0:T(8,128)(2,1)S(1)} %bitcast.13, bf16[12,400,128]{2,1,0:T(8,128)(2,1)S(1)} %get-tuple-element.51.orbit_ref, bf16[400,128]{1,0:T(8,128)(2,1)S(1)} %get-tuple-element.52.near_ref, ...), custom_call_target="tpu_custom_call" | custom-call | flops 983040000 | bytes 5000000 | tf_op jit(solution)/shard_map/exchange/pallas_call | solution.py:208
  117.8 4.5 %exchange.15.before_ref = f32[12,8,200]{2,1,0:T(8,128)S(1)} custom-call(bf16[200,800]{1,0:T(8,128)(2,1)S(1)} %collective-permute-done.12.x_ref.refs_6_, bf16[1536,800]{1,0:T(8,128)(2,1)S(1)} %bitcast.14, bf16[12,400,128]{2,1,0:T(8,128)(2,1)S(1)} %get-tuple-element.51.orbit_ref, bf16[400,128]{1,0:T(8,128)(2,1)S(1)} %get-tuple-element.52.near_ref, ...), custom_call_target="tpu_custom_call" | custom-call | flops 983040000 | bytes 5000000 | tf_op jit(solution)/shard_map/exchange/pallas_call | solution.py:208
  122.3 0.1 collective-permute-start.16
  122.4 3.5 %collective-permute-start.17 = (bf16[200,800]{1,0:T(8,128)(2,1)S(1)}, bf16[200,800]{1,0:T(8,128)(2,1)S(1)}, u32[]{:S(2)}, u32[]{:S(2)}) collective-permute-start(bf16[200,800]{1,0:T(8,128)(2,1)S(1)} %collective-permute-done.15.refs_14_), channel_id=1, source_target_pairs={{0,30},{1,31},{2,0},{3,1},{4,2},{5,3},{6,4},{7,5},{8,6},{9,7},{10,... | collective-permute-start | bytes 960008 | tf_op jit(solution)/shard_map/ppermute | solution.py:394
  125.9 4.5 %exchange.16.before_ref = f32[12,8,200]{2,1,0:T(8,128)S(1)} custom-call(bf16[200,800]{1,0:T(8,128)(2,1)S(1)} %collective-permute-done.14.x_ref.refs_7_, bf16[1536,800]{1,0:T(8,128)(2,1)S(1)} %bitcast.15, bf16[12,400,128]{2,1,0:T(8,128)(2,1)S(1)} %get-tuple-element.51.orbit_ref, bf16[400,128]{1,0:T(8,128)(2,1)S(1)} %get-tuple-element.52.near_ref, ...), custom_call_target="tpu_custom_call" | custom-call | flops 983040000 | bytes 5000000 | tf_op jit(solution)/shard_map/exchange/pallas_call | solution.py:208
  130.4 0.6 collective-permute-done.16.x_ref.refs_8_
  131.0 4.5 %exchange.17.refs_17_ = f32[12,8,200]{2,1,0:T(8,128)S(1)} custom-call(bf16[200,800]{1,0:T(8,128)(2,1)S(1)} %collective-permute-done.16.x_ref.refs_8_, bf16[1536,800]{1,0:T(8,128)(2,1)S(1)} %bitcast.16, bf16[12,400,128]{2,1,0:T(8,128)(2,1)S(1)} %get-tuple-element.51.orbit_ref, bf16[400,128]{1,0:T(8,128)(2,1)S(1)} %get-tuple-element.52.near_ref, ...), custom_call_target="tpu_custom_call" | custom-call | flops 983040000 | bytes 5000000 | tf_op jit(solution)/shard_map/exchange/pallas_call | solution.py:208
  135.5 7.6 %degree.3 = (f32[104,800]{1,0:T(8,128)S(1)}, f32[96,800]{1,0:T(8,128)S(1)}) custom-call(f32[16,2,200]{2,1,0:T(2,128)S(1)} %all_to_all.16.field_ref, bf16[200,800]{1,0:T(8,128)(2,1)S(1)} %copy-done.3, bf16[200,800]{1,0:T(8,128)(2,1)S(1)} %collective-permute-done.1.x_ref.refs_1_, bf16[200,800]{1,0:T(8,128)(2,1)} %collective-permute-done.3.x_ref.refs_2_, ...), custom_call_target="tpu_custom_call" | custom-call | flops 983040000 | bytes 6000000 | tf_op jit(solution)/shard_map/degree/pallas_call | solution.py:279
  143.1 0.1 collective-permute-start.18
  143.3 1.7 collective-permute-done.18.refs_17_
  144.9 7.4 %degree.4 = (f32[96,800]{1,0:T(8,128)S(1)}, f32[96,800]{1,0:T(8,128)S(1)}) custom-call(f32[16,2,200]{2,1,0:T(2,128)S(1)} %all_to_all.16.field_ref, bf16[200,800]{1,0:T(8,128)(2,1)S(1)} %copy-done.3, bf16[200,800]{1,0:T(8,128)(2,1)S(1)} %collective-permute-done.1.x_ref.refs_1_, bf16[200,800]{1,0:T(8,128)(2,1)} %collective-permute-done.3.x_ref.refs_2_, ...), custom_call_target="tpu_custom_call" | custom-call | flops 983040000 | bytes 6000000 | tf_op jit(solution)/shard_map/degree/pallas_call | solution.py:279
  152.4 0.2 collective-permute-start.19
  152.6 1.5 collective-permute-done.19.refs_17_
  154.1 7.4 %degree.5 = (f32[96,800]{1,0:T(8,128)S(1)}, f32[96,800]{1,0:T(8,128)S(1)}) custom-call(f32[16,2,200]{2,1,0:T(2,128)S(1)} %all_to_all.16.field_ref, bf16[200,800]{1,0:T(8,128)(2,1)S(1)} %copy-done.3, bf16[200,800]{1,0:T(8,128)(2,1)S(1)} %collective-permute-done.1.x_ref.refs_1_, bf16[200,800]{1,0:T(8,128)(2,1)} %collective-permute-done.3.x_ref.refs_2_, ...), custom_call_target="tpu_custom_call" | custom-call | flops 983040000 | bytes 6000000 | tf_op jit(solution)/shard_map/degree/pallas_call | solution.py:279
  161.5 0.3 collective-permute-start.20
  161.8 1.5 collective-permute-done.20.other_ref
  163.3 0.2 finish.1
  163.5 18.2 %all_to_all.17 = bf16[16,25,128]{2,1,0:T(8,128)(2,1)S(1)} all-to-all(bf16[16,25,128]{2,1,0:T(8,128)(2,1)S(1)} %finish.1), channel_id=1, replica_groups={{0,2,4,6,8,10,12,14,16,18,20,22,24,26,28,30},{1,3,5,7,9,11,13,15,17,19,..., dimensions={0} | all-to-all | bytes 204800 | tf_op jit(solution)/shard_map/all_to_all | solution.py:409
  181.8 0.1 reshape.15
  181.9 0.7 copy.10
  182.6 0.6 convert_reduce_fusion
  (35 shorter events, 0.1 us)
Async XLA Ops:
  0.6 21.3 %collective-permute-start.1 = (bf16[200,800]{1,0:T(8,128)(2,1)}, bf16[200,800]{1,0:T(8,128)(2,1)S(1)}, u32[]{:S(2)}, u32[]{:S(2)}) collective-permute-start(bf16[200,800]{1,0:T(8,128)(2,1)} %refs_0_.5), channel_id=1, source_target_pairs={{0,2},{1,3},{2,4},{3,5},{4,6},{5,7},{6,8},{7,9},{8,10},{9,11},{10,... | collective-permute-start | bytes 960008 | tf_op jit(solution)/shard_map/ppermute | solution.py:346
  2.9 19.1 %collective-permute-start.2 = (bf16[200,800]{1,0:T(8,128)(2,1)}, bf16[200,800]{1,0:T(8,128)(2,1)}, u32[]{:S(2)}, u32[]{:S(2)}) collective-permute-start(bf16[200,800]{1,0:T(8,128)(2,1)} %refs_0_.5), channel_id=1, source_target_pairs={{0,30},{1,31},{2,0},{3,1},{4,2},{5,3},{6,4},{7,5},{8,6},{9,7},{10,... | collective-permute-start | bytes 960008 | tf_op jit(solution)/shard_map/ppermute | solution.py:346
  13.4 16.3 %collective-permute-start = (bf16[200,800]{1,0:T(8,128)(2,1)}, bf16[200,800]{1,0:T(8,128)(2,1)}, u32[]{:S(2)}, u32[]{:S(2)}) collective-permute-start(bf16[200,800]{1,0:T(8,128)(2,1)} %refs_0_.5), channel_id=1, source_target_pairs={{0,1},{1,0},{2,3},{3,2},{4,5},{5,4},{6,7},{7,6},{8,9},{9,8},{10,11... | collective-permute-start | bytes 960008 | tf_op jit(solution)/shard_map/ppermute | solution.py:343
  13.4 1.7 copy-start.4
  16.4 10.0 %copy-start = (bf16[2,16,200,200]{3,2,1,0:T(8,128)(2,1)}, bf16[2,16,200,200]{3,2,1,0:T(8,128)(2,1)S(1)}, u32[]{:S(2)}) copy-start(bf16[2,16,200,200]{3,2,1,0:T(8,128)(2,1)S(1)} %split.1.cores_ref.cores_any) | copy-start | bytes 7680004
  21.9 12.2 %collective-permute-start.3 = (bf16[200,800]{1,0:T(8,128)(2,1)S(1)}, bf16[200,800]{1,0:T(8,128)(2,1)}, u32[]{:S(2)}, u32[]{:S(2)}) collective-permute-start(bf16[200,800]{1,0:T(8,128)(2,1)S(1)} %collective-permute-done.1.x_ref.refs_1_), channel_id=1, source_target_pairs={{0,2},{1,3},{2,4},{3,5},{4,6},{5,7},{6,8},{7,9},{8,10},{9,11},{10,... | collective-permute-start | bytes 960008 | tf_op jit(solution)/shard_map/ppermute | solution.py:346
  21.9 12.2 %collective-permute-start.4 = (bf16[200,800]{1,0:T(8,128)(2,1)}, bf16[200,800]{1,0:T(8,128)(2,1)}, u32[]{:S(2)}, u32[]{:S(2)}) collective-permute-start(bf16[200,800]{1,0:T(8,128)(2,1)} %collective-permute-done.2.refs_9_), channel_id=1, source_target_pairs={{0,30},{1,31},{2,0},{3,1},{4,2},{5,3},{6,4},{7,5},{8,6},{9,7},{10,... | collective-permute-start | bytes 960008 | tf_op jit(solution)/shard_map/ppermute | solution.py:346
  26.4 3.3 %copy-start.3 = (bf16[200,800]{1,0:T(8,128)(2,1)S(1)}, bf16[200,800]{1,0:T(8,128)(2,1)}, u32[]{:S(2)}) copy-start(bf16[200,800]{1,0:T(8,128)(2,1)} %refs_0_.5) | copy-start | bytes 960004
  26.4 53.8 %collective-permute-start.9 = (bf16[1,16,200,200]{3,2,1,0:T(8,128)(2,1)}, bf16[1,16,200,200]{3,2,1,0:T(8,128)(2,1)}, u32[]{:S(2)}, u32[]{:S(2)}) collective-permute-start(bf16[1,16,200,200]{3,2,1,0:T(8,128)(2,1)} %slice.20), channel_id=1, source_target_pairs={{0,1},{1,0},{2,3},{3,2},{4,5},{5,4},{6,7},{7,6},{8,9},{9,8},{10,11... | collective-permute-start | bytes 3840008 | tf_op jit(solution)/shard_map/ppermute | solution.py:343
  29.7 1.4 copy-start.2
  31.2 27.7 %copy-start.1 = (bf16[2,16,200,200]{3,2,1,0:T(8,128)(2,1)S(1)}, bf16[2,16,200,200]{3,2,1,0:T(8,128)(2,1)}, u32[]{:S(2)}) copy-start(bf16[2,16,200,200]{3,2,1,0:T(8,128)(2,1)} %copy-done) | copy-start | bytes 7680004
  31.2 27.7 %copy-start.5 = (s32[200,12]{0,1:T(8,128)S(1)}, s32[200,12]{0,1:T(8,128)}, u32[]{:S(2)}) copy-start(s32[200,12]{0,1:T(8,128)} %param.9) | copy-start | bytes 28804
  55.6 3.3 %collective-permute-start.5 = (bf16[16,16,200]{2,1,0:T(8,128)(2,1)S(1)}, bf16[16,16,200]{2,1,0:T(8,128)(2,1)S(1)}, u32[]{:S(2)}, u32[]{:S(2)}) collective-permute-start(bf16[16,16,200]{2,1,0:T(8,128)(2,1)S(1)} %all_to_all.15.mine_ref), channel_id=1, source_target_pairs={{0,1},{1,0},{2,3},{3,2},{4,5},{5,4},{6,7},{7,6},{8,9},{9,8},{10,11... | collective-permute-start | bytes 307208 | tf_op jit(solution)/shard_map/ppermute | solution.py:343
  55.6 21.5 %collective-permute-start.6 = (bf16[200,800]{1,0:T(8,128)(2,1)}, bf16[200,800]{1,0:T(8,128)(2,1)S(1)}, u32[]{:S(2)}, u32[]{:S(2)}) collective-permute-start(bf16[200,800]{1,0:T(8,128)(2,1)} %collective-permute-done.3.x_ref.refs_2_), channel_id=1, source_target_pairs={{0,2},{1,3},{2,4},{3,5},{4,6},{5,7},{6,8},{7,9},{8,10},{9,11},{10,... | collective-permute-start | bytes 960008 | tf_op jit(solution)/shard_map/ppermute | solution.py:346
  57.5 19.5 %collective-permute-start.7 = (bf16[200,800]{1,0:T(8,128)(2,1)}, bf16[200,800]{1,0:T(8,128)(2,1)S(1)}, u32[]{:S(2)}, u32[]{:S(2)}) collective-permute-start(bf16[200,800]{1,0:T(8,128)(2,1)} %collective-permute-done.4.refs_10_), channel_id=1, source_target_pairs={{0,30},{1,31},{2,0},{3,1},{4,2},{5,3},{6,4},{7,5},{8,6},{9,7},{10,... | collective-permute-start | bytes 960008 | tf_op jit(solution)/shard_map/ppermute | solution.py:346
  77.0 10.1 %collective-permute-start.8 = (bf16[200,800]{1,0:T(8,128)(2,1)S(1)}, bf16[200,800]{1,0:T(8,128)(2,1)S(1)}, u32[]{:S(2)}, u32[]{:S(2)}) collective-permute-start(bf16[200,800]{1,0:T(8,128)(2,1)S(1)} %collective-permute-done.6.x_ref.refs_3_), channel_id=1, source_target_pairs={{0,2},{1,3},{2,4},{3,5},{4,6},{5,7},{6,8},{7,9},{8,10},{9,11},{10,... | collective-permute-start | bytes 960008 | tf_op jit(solution)/shard_map/ppermute | solution.py:346
  77.8 13.9 %collective-permute-start.11 = (bf16[200,800]{1,0:T(8,128)(2,1)S(1)}, bf16[200,800]{1,0:T(8,128)(2,1)S(1)}, u32[]{:S(2)}, u32[]{:S(2)}) collective-permute-start(bf16[200,800]{1,0:T(8,128)(2,1)S(1)} %collective-permute-done.7.refs_11_), channel_id=1, source_target_pairs={{0,30},{1,31},{2,0},{3,1},{4,2},{5,3},{6,4},{7,5},{8,6},{9,7},{10,... | collective-permute-start | bytes 960008 | tf_op jit(solution)/shard_map/ppermute | solution.py:346
  87.1 13.5 %collective-permute-start.10 = (bf16[200,800]{1,0:T(8,128)(2,1)S(1)}, bf16[200,800]{1,0:T(8,128)(2,1)S(1)}, u32[]{:S(2)}, u32[]{:S(2)}) collective-permute-start(bf16[200,800]{1,0:T(8,128)(2,1)S(1)} %collective-permute-done.8.x_ref.refs_4_), channel_id=1, source_target_pairs={{0,2},{1,3},{2,4},{3,5},{4,6},{5,7},{6,8},{7,9},{8,10},{9,11},{10,... | collective-permute-start | bytes 960008 | tf_op jit(solution)/shard_map/ppermute | solution.py:389
  91.7 13.6 %collective-permute-start.13 = (bf16[200,800]{1,0:T(8,128)(2,1)S(1)}, bf16[200,800]{1,0:T(8,128)(2,1)S(1)}, u32[]{:S(2)}, u32[]{:S(2)}) collective-permute-start(bf16[200,800]{1,0:T(8,128)(2,1)S(1)} %collective-permute-done.11.refs_12_), channel_id=1, source_target_pairs={{0,30},{1,31},{2,0},{3,1},{4,2},{5,3},{6,4},{7,5},{8,6},{9,7},{10,... | collective-permute-start | bytes 960008 | tf_op jit(solution)/shard_map/ppermute | solution.py:394
  100.6 12.4 %collective-permute-start.12 = (bf16[200,800]{1,0:T(8,128)(2,1)S(1)}, bf16[200,800]{1,0:T(8,128)(2,1)S(1)}, u32[]{:S(2)}, u32[]{:S(2)}) collective-permute-start(bf16[200,800]{1,0:T(8,128)(2,1)S(1)} %collective-permute-done.10.x_ref.refs_5_), channel_id=1, source_target_pairs={{0,2},{1,3},{2,4},{3,5},{4,6},{5,7},{6,8},{7,9},{8,10},{9,11},{10,... | collective-permute-start | bytes 960008 | tf_op jit(solution)/shard_map/ppermute | solution.py:389
  105.3 12.4 %collective-permute-start.15 = (bf16[200,800]{1,0:T(8,128)(2,1)S(1)}, bf16[200,800]{1,0:T(8,128)(2,1)S(1)}, u32[]{:S(2)}, u32[]{:S(2)}) collective-permute-start(bf16[200,800]{1,0:T(8,128)(2,1)S(1)} %collective-permute-done.13.refs_13_), channel_id=1, source_target_pairs={{0,30},{1,31},{2,0},{3,1},{4,2},{5,3},{6,4},{7,5},{8,6},{9,7},{10,... | collective-permute-start | bytes 960008 | tf_op jit(solution)/shard_map/ppermute | solution.py:394
  113.1 9.2 %collective-permute-start.14 = (bf16[200,800]{1,0:T(8,128)(2,1)S(1)}, bf16[200,800]{1,0:T(8,128)(2,1)S(1)}, u32[]{:S(2)}, u32[]{:S(2)}) collective-permute-start(bf16[200,800]{1,0:T(8,128)(2,1)S(1)} %collective-permute-done.12.x_ref.refs_6_), channel_id=1, source_target_pairs={{0,2},{1,3},{2,4},{3,5},{4,6},{5,7},{6,8},{7,9},{8,10},{9,11},{10,... | collective-permute-start | bytes 960008 | tf_op jit(solution)/shard_map/ppermute | solution.py:389
  122.3 8.7 %collective-permute-start.16 = (bf16[200,800]{1,0:T(8,128)(2,1)S(1)}, bf16[200,800]{1,0:T(8,128)(2,1)S(1)}, u32[]{:S(2)}, u32[]{:S(2)}) collective-permute-start(bf16[200,800]{1,0:T(8,128)(2,1)S(1)} %collective-permute-done.14.x_ref.refs_7_), channel_id=1, source_target_pairs={{0,2},{1,3},{2,4},{3,5},{4,6},{5,7},{6,8},{7,9},{8,10},{9,11},{10,... | collective-permute-start | bytes 960008 | tf_op jit(solution)/shard_map/ppermute | solution.py:389
  122.4 13.1 %collective-permute-start.17 = (bf16[200,800]{1,0:T(8,128)(2,1)S(1)}, bf16[200,800]{1,0:T(8,128)(2,1)S(1)}, u32[]{:S(2)}, u32[]{:S(2)}) collective-permute-start(bf16[200,800]{1,0:T(8,128)(2,1)S(1)} %collective-permute-done.15.refs_14_), channel_id=1, source_target_pairs={{0,30},{1,31},{2,0},{3,1},{4,2},{5,3},{6,4},{7,5},{8,6},{9,7},{10,... | collective-permute-start | bytes 960008 | tf_op jit(solution)/shard_map/ppermute | solution.py:394
  143.1 1.8 collective-permute-start.18
  152.4 1.8 collective-permute-start.19
  161.5 1.8 collective-permute-start.20
